TPU v7x, 256 devices: a whole 4x4x8 slice. The times are simulated.
256 devices in a mesh: dp: 64 (over x, z_lo, y, core), mp: 4 (over z_hi).
Axes of the slice: x: 4, y: 4, z: 8 (z_hi: 4, z_lo: 2; z = z_hi * 2 + z_lo), core: 2. Of those that a mesh axis runs over, the one named last changes fastest.
Arguments:
- pooled: bfloat16 [16384, 3584], P('dp', 'mp'), may hold values from -4 to 4
- w_out: bfloat16 [3584, 3584], P('mp'), may hold values from -0.028931878 to 0.028931878
- assignments: int32 [16384], P('dp'), may hold values from 0 to 4095
- ema_sums: float32 [4096, 3584], P('mp', 'dp'), may hold values from -0.40089186 to 0.40089186
- ema_counts: float32 [4096], P('mp'), may hold values from 1 to 8
Outputs:
- distances: float32 [16384, 4096], P('dp', 'mp')
- new_sums: float32 [4096, 3584], P('mp', 'dp')
- new_counts: float32 [4096], P('mp')
- new_centroids: bfloat16 [4096, 3584], P('mp', 'dp')
All inputs are finite; a program needn't handle non-finite values.
Results may differ from a plain program's by a relative error of at most 0.0011.
Values may be sent and summed in bfloat16 or wider, within the bound.
No kernel may reach another device: no remote copies, remote signals or barrier semaphores. Data moves between devices by JAX's collectives and lax.ppermute only.
A program may use at most 64 MiB of HBM per device.

v0:
```python
import jax
import jax.numpy as jnp
from jax import lax
from jax.experimental import pallas as pl
from jax.experimental.pallas import tpu as pltpu
from jax.sharding import PartitionSpec as P


EPSILON = 1e-06
EMA_DECAY = 0.9
SCALE = 64.0
MP = 4
GRID = (4, 2, 4, 2)
LANES = 256


def mp_shift(value, step):
    return lax.ppermute(value, "mp", [(i, (i + step) % MP) for i in range(MP)])


def after(values, *others):
    return lax.optimization_barrier((values, others))[0]


def dp_index(place):
    index = 0
    for size, at in zip(GRID, place):
        index = index * size + at % size
    return index


def dp_shift(value, dim, step):
    pairs = []
    for index in range(64):
        rest, place = index, []
        for size in reversed(GRID):
            place.insert(0, rest % size)
            rest //= size
        moved = list(place)
        moved[dim] += step
        pairs.append((index, dp_index(moved)))
    return lax.ppermute(value, "dp", pairs)


def gather_line(piece, hold):
    pair = jnp.stack([piece, after(dp_shift(piece, 1, 1), hold)])
    return [pair] + [dp_shift(pair, 2, -step) for step in (1, 2, 3)]


def gather_plane(line, hold):
    line = jnp.stack(after(line, hold))
    return [line] + [dp_shift(line, 0, -step) for step in (1, 2, 3)]


def gather_table(plane, hold):
    plane = jnp.stack(after(plane, hold))
    return plane, dp_shift(plane, 3, 1)


def table_order(index):
    my = (index // 16, index // 8 % 2, index // 2 % 4, index % 2)
    i = jnp.arange(64, dtype=jnp.int32)
    x, low, y, core = (my[0] + i // 8) % 4, (my[1] + i) % 2, (my[2] + i // 2) % 4, (my[3] + i // 32) % 2
    blocks = ((x * 2 + low) * 4 + y) * 2 + core
    x, low, y, core = (i // 16 - my[0]) % 4, (i // 8 - my[1]) % 2, (i // 2 - my[2]) % 4, (i - my[3]) % 2
    entries = ((core * 4 + x) * 4 + y) * 2 + low
    return blocks.astype(jnp.int32), entries.astype(jnp.int32)


def place_kernel(at_ref, *refs):
    pieces, out_ref = refs[:-1], refs[-1]
    rows = pieces[0].shape[0]
    for i, piece in enumerate(pieces):
        out_ref[pl.ds(pl.multiple_of(at_ref[i], 64), rows), :] = piece[...]


def put_in_place(at, pieces):
    rows, docs = pieces[0].shape
    total = rows * len(pieces)
    whole = pl.BlockSpec(memory_space=pltpu.VMEM)
    return pl.pallas_call(
        place_kernel,
        grid_spec=pltpu.PrefetchScalarGridSpec(
            num_scalar_prefetch=1, grid=(), in_specs=[whole] * len(pieces), out_specs=whole
        ),
        out_shape=jax.ShapeDtypeStruct((total, docs), jnp.bfloat16),
        cost_estimate=pl.CostEstimate(flops=1_000_000, bytes_accessed=4 * total * docs, transcendentals=0),
        name="put_in_place",
    )(at, *pieces)


def order_kernel(blocks_ref, whole_ref, order_ref, norms_ref):
    docs = whole_ref.shape[1]
    cols, tall = whole_ref.shape[0] // 64, order_ref.shape[0] // 64
    zeros = jnp.zeros((tall - cols, docs), jnp.bfloat16)
    norms = jnp.zeros((8, docs), jnp.float32)
    for i in range(64):
        block = whole_ref[pl.ds(pl.multiple_of(blocks_ref[i] * cols, 8), cols), :]
        wide = block.astype(jnp.float32)
        norms += jnp.sum((wide * wide).reshape(cols // 8, 8, docs), axis=0)
        order_ref[i * tall : i * tall + cols, :] = block
        order_ref[i * tall + cols : (i + 1) * tall, :] = zeros
    norms_ref[...] = jnp.sum(norms, axis=0, keepdims=True)


def put_in_order(blocks, whole):
    rows, docs = whole.shape
    vmem = pl.BlockSpec(memory_space=pltpu.VMEM)
    return pl.pallas_call(
        order_kernel,
        grid_spec=pltpu.PrefetchScalarGridSpec(num_scalar_prefetch=1, grid=(), in_specs=[vmem], out_specs=[vmem] * 2),
        out_shape=[
            jax.ShapeDtypeStruct((rows + 64 * 8, docs), jnp.bfloat16),
            jax.ShapeDtypeStruct((1, docs), jnp.float32),
        ],
        cost_estimate=pl.CostEstimate(flops=3_000_000, bytes_accessed=4 * rows * docs, transcendentals=0),
        name="put_in_order",
    )(blocks, whole)


def sums_kernel(first_ref, entries_ref, codes_ref, cols_ref, ema_ref, counts_ref, sums_out, counts_out, means_out, total):
    group, rows, docs = cols_ref.shape
    tall = rows + 8
    blocks = total.shape[1] // LANES

    @pl.when(pl.program_id(0) == 0)
    def _():
        total[...] = jnp.zeros_like(total)

    assign = []
    for i in range(group):
        codes = codes_ref[entries_ref[pl.program_id(0) * group + i]].astype(jnp.float32)
        assign.append(codes[0:1, :docs] * 64.0 + codes[0:1, docs:])
    assign = jnp.concatenate(assign, axis=1).astype(jnp.int32) - first_ref[0]
    low = assign & (LANES - 1)
    high = assign - low
    ids = lax.broadcasted_iota(jnp.int32, (LANES, docs * group), 0)
    hot = jnp.where(low == ids, 1.0, 0.0).astype(jnp.bfloat16)
    cols = jnp.concatenate([cols_ref[i] for i in range(group)], axis=1)
    ones = jnp.ones((8, docs * group), jnp.bfloat16)
    cols = jnp.concatenate([cols, ones], axis=0)
    picked = []
    for b in range(blocks):
        mask = jnp.where(high == b * LANES, 1.0, 0.0).astype(jnp.bfloat16)
        picked.append(cols * mask)
    picked = jnp.concatenate(picked, axis=0)
    got = lax.dot_general(picked, hot, (((1,), (1,)), ((), ())), preferred_element_type=jnp.float32)
    for b in range(blocks):
        total[:, b * LANES : (b + 1) * LANES] += got[b * tall : (b + 1) * tall]

    @pl.when(pl.program_id(0) == pl.num_programs(0) - 1)
    def _():
        counts = EMA_DECAY * counts_ref[...] + (1.0 - EMA_DECAY) * total[rows : rows + 1]
        sums = EMA_DECAY * ema_ref[...] + (1.0 - EMA_DECAY) * total[:rows]
        counts_out[...] = counts
        sums_out[...] = sums
        means_out[...] = (sums / counts).astype(jnp.bfloat16)


def new_state(first, entries, codes, cols, ema_sums, ema_counts):
    shards, rows, docs = cols.shape
    width = ema_counts.shape[1]
    group = 8

    def all_of(shape):
        return pl.BlockSpec(shape, lambda i, f, e: (0,) * len(shape))

    return pl.pallas_call(
        sums_kernel,
        grid_spec=pltpu.PrefetchScalarGridSpec(
            num_scalar_prefetch=2,
            grid=(shards // group,),
            in_specs=[
                all_of(codes.shape),
                pl.BlockSpec((group, rows, docs), lambda i, f, e: (i, 0, 0)),
                all_of((rows, width)),
                all_of((1, width)),
            ],
            out_specs=[all_of((rows, width)), all_of((1, width)), all_of((rows, width))],
            scratch_shapes=[pltpu.VMEM((rows + 8, width), jnp.float32)],
        ),
        out_shape=[
            jax.ShapeDtypeStruct((rows, width), jnp.float32),
            jax.ShapeDtypeStruct((1, width), jnp.float32),
            jax.ShapeDtypeStruct((rows, width), jnp.bfloat16),
        ],
        cost_estimate=pl.CostEstimate(
            flops=2 * width * shards * docs * rows, bytes_accessed=2 * shards * rows * docs, transcendentals=0
        ),
        name="new_state",
    )(first, entries, codes, cols, ema_sums, ema_counts)


def step(pooled, w_out, assignments, ema_sums, ema_counts):
    me = lax.axis_index("mp")
    index = lax.axis_index("dp")
    blocks, entries = table_order(index)
    docs, depth = pooled.shape
    half_docs, half = docs // 2, depth // 2
    width, feature_cols = ema_sums.shape
    shards = lax.axis_size("dp")
    f16 = jnp.float16

    def partial(step):
        w = lax.dynamic_slice_in_dim(w_out, (me + step) % MP * depth, depth, 1)
        return jnp.dot(pooled, w, preferred_element_type=jnp.float32) * SCALE

    far = partial(2).astype(f16)
    up = mp_shift(far[:half_docs], 1)
    down = mp_shift(far[half_docs:], -1)
    sums_t = ema_sums.T
    centers = (sums_t / ema_counts[None, :]).astype(jnp.bfloat16)
    pair = jnp.stack([assignments // 64, assignments % 64]).astype(jnp.bfloat16).reshape(1, 2 * docs)
    extra = jnp.pad(pair, ((0, 7), (0, width - 2 * docs)))
    centers = after(jnp.concatenate([centers, extra]), far)
    ahead, behind = partial(1), partial(-1)
    low_a, top_b = ahead[half_docs:].astype(f16), behind[:half_docs].astype(f16)
    line = gather_line(centers, (low_a, top_b))
    near = (low_a, top_b)
    low_a, top_b = mp_shift(low_a, 1), mp_shift(top_b, -1)
    mine = partial(0)
    up, down = after((up, down), near, mine)
    top_a = (ahead[:half_docs] + up.astype(jnp.float32)).astype(f16)
    low_b = (behind[half_docs:] + down.astype(jnp.float32)).astype(f16)
    plane = gather_plane(line, (top_a, low_b))
    top_a, low_b = mp_shift(top_a, 1), mp_shift(low_b, -1)
    top = mine[:half_docs] + top_a.astype(jnp.float32) + top_b.astype(jnp.float32)
    low = mine[half_docs:] + low_a.astype(jnp.float32) + low_b.astype(jnp.float32)
    share = jnp.concatenate([top, low]).T.astype(f16)
    first_half, second_half = share[:half], share[half:]
    a_first = mp_shift(first_half, 1)
    b_second = mp_shift(second_half, -1)
    a_second = mp_shift(second_half, 1)
    b_first = mp_shift(first_half, -1)
    c_first = mp_shift(a_first, 1)
    c_second = mp_shift(b_second, -1)

    tables = gather_table(plane, (a_first, b_second, a_second, b_first))
    blocks, entries = table_order(index)
    parts = [first_half, second_half, b_first, b_second, c_first, c_second, a_first, a_second]
    i = jnp.arange(len(parts), dtype=jnp.int32)
    at = ((me + i // 2) % MP * depth + i % 2 * half).astype(jnp.int32)
    wide = [p.astype(jnp.float32) for p in parts]
    squares = sum(jnp.sum(p * p, axis=0) for p in wide)
    inverse = lax.rsqrt(squares + EPSILON * SCALE * SCALE)
    pieces = [(p * inverse[None, :]).astype(jnp.bfloat16) for p in wide]
    embedded = put_in_place(at, pieces)
    received = lax.all_to_all(
        embedded.reshape(shards, feature_cols, docs), "dp", split_axis=0, concat_axis=0, tiled=True
    )
    ordered, doc_norms = put_in_order(blocks, embedded)
    tables = [t.reshape(shards // 2, feature_cols + 8, width) for t in tables]
    codes = jnp.concatenate([t[:, feature_cols:, : 2 * docs] for t in tables])
    real = lax.broadcasted_iota(jnp.int32, tables[0].shape, 1) < feature_cols
    center_norms, products = 0.0, 0.0
    for i, table in enumerate(tables):
        wide = jnp.where(real, table.astype(jnp.float32), 0.0)
        center_norms = center_norms + jnp.sum(wide * wide, axis=(0, 1))
        rows = table.reshape(-1, width)
        part = ordered[i * rows.shape[0] : (i + 1) * rows.shape[0]]
        products = products + lax.dot_general(part, rows, (((0,), (0,)), ((), ())), preferred_element_type=jnp.float32)
    distances = doc_norms[0][:, None] + center_norms[None, :] - 2.0 * products
    received, distances, codes = lax.optimization_barrier((received, distances, codes))
    new_sums, new_counts, new_centroids = new_state(
        (me * width).reshape(1), entries, codes, received, sums_t, ema_counts[None, :]
    )
    return distances, new_sums.T, new_counts[0], new_centroids.T


def solution(mesh):
    return jax.shard_map(
        step,
        mesh=mesh,
        in_specs=(P("dp", "mp"), P("mp", None), P("dp"), P("mp", "dp"), P("mp")),
        out_specs=(P("dp", "mp"), P("mp", "dp"), P("mp"), P("mp", "dp")),
        check_vma=False,
    )
```

profile of v0, /device:TPU:1, one launch (start us, length us, event | category | flops | bytes accessed | tf_op | source)
XLA Modules:
  0.0 162.6 jit_solution(3999155898322186426)
XLA Ops:
  4.5 3.8 %collective-permute-start = (f16[128,896]{0,1:T(8,128)(2,1)}, f16[128,896]{0,1:T(8,128)(2,1)S(1)}, u32[]{:S(2)}, u32[]{:S(2)}) collective-permute-start(f16[128,896]{0,1:T(8,128)(2,1)} %get-tuple-element.55), channel_id=1, source_target_pairs={{0,1},{1,2},{2,3},{3,0},{4,5},{5,6},{6,7},{7,4},{8,9},{9,10},{10,1... | collective-permute-start | bytes 688136 | tf_op jit(solution)/shard_map/ppermute | solution.py:18
  8.4 3.0 %collective-permute-start.1 = (f16[128,896]{0,1:T(8,128)(2,1)S(1)}, f16[128,896]{0,1:T(8,128)(2,1)}, u32[]{:S(2)}, u32[]{:S(2)}) collective-permute-start(f16[128,896]{0,1:T(8,128)(2,1)S(1)} %get-tuple-element.54), channel_id=1, source_target_pairs={{0,3},{1,0},{2,1},{3,2},{4,7},{5,4},{6,5},{7,6},{8,11},{9,8},{10,9... | collective-permute-start | bytes 688136 | tf_op jit(solution)/shard_map/ppermute | solution.py:18
  16.8 2.4 %collective-permute-start.3 = (f16[128,896]{0,1:T(8,128)(2,1)}, f16[128,896]{0,1:T(8,128)(2,1)S(1)}, u32[]{:S(2)}, u32[]{:S(2)}) collective-permute-start(f16[128,896]{0,1:T(8,128)(2,1)} %slice_convert_fusion), channel_id=1, source_target_pairs={{0,3},{1,0},{2,1},{3,2},{4,7},{5,4},{6,5},{7,6},{8,11},{9,8},{10,9... | collective-permute-start | bytes 688136 | tf_op jit(solution)/shard_map/ppermute | solution.py:18
  24.1 6.3 %collective-permute-done.12 = bf16[64,1024]{1,0:T(8,128)(2,1)S(1)} collective-permute-done((bf16[64,1024]{1,0:T(8,128)(2,1)S(1)}, bf16[64,1024]{1,0:T(8,128)(2,1)S(1)}, u32[]{:S(2)}, u32[]{:S(2)}) %collective-permute-start.12) | collective-permute-done | bytes 131104 | tf_op jit(solution)/shard_map/ppermute | solution.py:42
  30.4 2.8 %collective-permute-start.13 = (bf16[2,64,1024]{2,1,0:T(8,128)(2,1)S(1)}, bf16[2,64,1024]{2,1,0:T(8,128)(2,1)S(1)}, u32[]{:S(2)}, u32[]{:S(2)}) collective-permute-start(bf16[2,64,1024]{2,1,0:T(8,128)(2,1)S(1)} %pad_maximum_fusion.3), channel_id=1, source_target_pairs={{0,24},{4,28},{8,0},{12,4},{16,8},{20,12},{24,16},{28,20},{32,56},... | collective-permute-start | bytes 786440 | tf_op jit(solution)/shard_map/ppermute | solution.py:42
  35.3 3.0 %collective-permute-done.13 = bf16[2,64,1024]{2,1,0:T(8,128)(2,1)S(1)} collective-permute-done((bf16[2,64,1024]{2,1,0:T(8,128)(2,1)S(1)}, bf16[2,64,1024]{2,1,0:T(8,128)(2,1)S(1)}, u32[]{:S(2)}, u32[]{:S(2)}) %collective-permute-start.13) | collective-permute-done | bytes 262176 | tf_op jit(solution)/shard_map/ppermute | solution.py:42
  38.3 2.6 %collective-permute-start.5 = (f16[128,896]{0,1:T(8,128)(2,1)S(1)}, f16[128,896]{0,1:T(8,128)(2,1)S(1)}, u32[]{:S(2)}, u32[]{:S(2)}) collective-permute-start(f16[128,896]{0,1:T(8,128)(2,1)S(1)} %fusion.57), channel_id=1, source_target_pairs={{0,3},{1,0},{2,1},{3,2},{4,7},{5,4},{6,5},{7,6},{8,11},{9,8},{10,9... | collective-permute-start | bytes 688136 | tf_op jit(solution)/shard_map/ppermute | solution.py:18
  41.0 7.6 %collective-permute-done.15 = bf16[2,64,1024]{2,1,0:T(8,128)(2,1)S(1)} collective-permute-done((bf16[2,64,1024]{2,1,0:T(8,128)(2,1)S(1)}, bf16[2,64,1024]{2,1,0:T(8,128)(2,1)S(1)}, u32[]{:S(2)}, u32[]{:S(2)}) %collective-permute-start.15) | collective-permute-done | bytes 262176 | tf_op jit(solution)/shard_map/ppermute | solution.py:42
  48.7 2.5 %collective-permute-start.16 = (bf16[4,2,64,1024]{3,2,1,0:T(8,128)(2,1)S(1)}, bf16[4,2,64,1024]{3,2,1,0:T(8,128)(2,1)S(1)}, u32[]{:S(2)}, u32[]{:S(2)}) collective-permute-start(bf16[4,2,64,1024]{3,2,1,0:T(8,128)(2,1)S(1)} %pad_maximum_fusion.1), channel_id=1, source_target_pairs={{0,192},{4,196},{8,200},{12,204},{16,208},{20,212},{24,216},{28,22... | collective-permute-start | bytes 3145736 | tf_op jit(solution)/shard_map/ppermute | solution.py:42
  52.9 3.6 %collective-permute-start.6 = (f16[448,256]{1,0:T(8,128)(2,1)S(1)}, f16[448,256]{1,0:T(8,128)(2,1)S(1)}, u32[]{:S(2)}, u32[]{:S(2)}) collective-permute-start(f16[448,256]{1,0:T(8,128)(2,1)S(1)} %get-tuple-element.52), channel_id=1, source_target_pairs={{0,3},{1,0},{2,1},{3,2},{4,7},{5,4},{6,5},{7,6},{8,11},{9,8},{10,9... | collective-permute-start | bytes 688136 | tf_op jit(solution)/shard_map/ppermute | solution.py:18
  56.4 6.9 %collective-permute-done.11 = f16[448,256]{1,0:T(8,128)(2,1)S(1)} collective-permute-done((f16[448,256]{1,0:T(8,128)(2,1)S(1)}, f16[448,256]{1,0:T(8,128)(2,1)S(1)}, u32[]{:S(2)}, u32[]{:S(2)}) %collective-permute-start.11) | collective-permute-done | bytes 229408 | tf_op jit(solution)/shard_map/ppermute | solution.py:18
  65.7 10.2 %collective-permute-done.7 = f16[448,256]{1,0:T(8,128)(2,1)S(1)} collective-permute-done((f16[448,256]{1,0:T(8,128)(2,1)S(1)}, f16[448,256]{1,0:T(8,128)(2,1)S(1)}, u32[]{:S(2)}, u32[]{:S(2)}) %collective-permute-start.7) | collective-permute-done | bytes 229408 | tf_op jit(solution)/shard_map/ppermute | solution.py:18
  76.7 23.6 %collective-permute-done.18 = bf16[4,2,64,1024]{3,2,1,0:T(8,128)(2,1)S(1)} collective-permute-done((bf16[4,2,64,1024]{3,2,1,0:T(8,128)(2,1)S(1)}, bf16[4,2,64,1024]{3,2,1,0:T(8,128)(2,1)S(1)}, u32[]{:S(2)}, u32[]{:S(2)}) %collective-permute-start.18) | collective-permute-done | bytes 1048608 | tf_op jit(solution)/shard_map/ppermute | solution.py:42
  100.3 2.4 %pad_maximum_fusion = bf16[4,4,2,64,1024]{4,3,2,1,0:T(8,128)(2,1)} fusion(bf16[1,4,2,64,1024]{4,3,2,1,0:T(8,128)(2,1)S(1)} %bitcast.50, bf16[1,4,2,64,1024]{4,3,2,1,0:T(8,128)(2,1)S(1)} %bitcast.48, bf16[1,4,2,64,1024]{4,3,2,1,0:T(8,128)(2,1)S(1)} %bitcast.46, bf16[1,4,2,64,1024]{4,3,2,1,0:T(8,128)(2,1)S(1)} %bitcast.44), kind=kLoop, calls=%fused_computation.2 | loop fusion | flops 6291456 | bytes 8388608 | tf_op jit(solution)/shard_map/stack | solution.py:56
  103.9 3.6 %collective-permute-start.10 = (f16[448,256]{1,0:T(8,128)(2,1)S(1)}, f16[448,256]{1,0:T(8,128)(2,1)S(1)}, u32[]{:S(2)}, u32[]{:S(2)}) collective-permute-start(f16[448,256]{1,0:T(8,128)(2,1)S(1)} %collective-permute-done.7), channel_id=1, source_target_pairs={{0,3},{1,0},{2,1},{3,2},{4,7},{5,4},{6,5},{7,6},{8,11},{9,8},{10,9... | collective-permute-start | bytes 688136 | tf_op jit(solution)/shard_map/ppermute | solution.py:18
  107.8 9.2 %collective-permute-done.9 = f16[448,256]{1,0:T(8,128)(2,1)S(1)} collective-permute-done((f16[448,256]{1,0:T(8,128)(2,1)S(1)}, f16[448,256]{1,0:T(8,128)(2,1)S(1)}, u32[]{:S(2)}, u32[]{:S(2)}) %collective-permute-start.9) | collective-permute-done | bytes 229408 | tf_op jit(solution)/shard_map/ppermute | solution.py:18
  119.3 3.6 %put_in_place.1.whole_ref = bf16[3584,256]{1,0:T(8,128)(2,1)} custom-call(s32[8]{0:T(128)} %fusion.72.at_ref, bf16[448,256]{1,0:T(8,128)(2,1)} %get-tuple-element.51.refs_0_, bf16[448,256]{1,0:T(8,128)(2,1)} %get-tuple-element.50.refs_1_, bf16[448,256]{1,0:T(8,128)(2,1)} %get-tuple-element.63.refs_2_, bf16[448,256]{1,0:T(8,128)(2,1)} %get-tuple-element.62.refs_3_, ...), custom_call_target="tpu_custom_call" | custom-call | flops 1000000 | bytes 3670016 | tf_op jit(solution)/shard_map/put_in_place/pallas_call | solution.py:81
  122.8 5.3 %all-to-all-start = ((bf16[64,56,256]{2,1,0:T(8,128)(2,1)}), bf16[64,56,256]{2,1,0:T(8,128)(2,1)}, u32[]{:S(2)}, u32[]{:S(2)}) async-start(bf16[64,56,256]{2,1,0:T(8,128)(2,1)} %bitcast.43), calls=%async_computation | async-start | bytes 3670016 | tf_op jit(solution)/shard_map/all_to_all | solution.py:248
  128.8 3.7 %put_in_order.1 = (bf16[4096,256]{1,0:T(8,128)(2,1)}, f32[1,256]{1,0:T(1,128)}) custom-call(s32[64]{0:T(128)} %get-tuple-element.64.blocks_ref, bf16[3584,256]{1,0:T(8,128)(2,1)} %put_in_place.1.whole_ref), custom_call_target="tpu_custom_call" | custom-call | flops 3000000 | bytes 3670016 | tf_op jit(solution)/shard_map/put_in_order/pallas_call | solution.py:109
  133.7 3.8 %fusion.37 = f32[256,1024]{1,0:T(8,128)S(1)} fusion(bf16[2048,1024]{1,0:T(8,128)(2,1)} %bitcast.18, bf16[4096,256]{1,0:T(8,128)(2,1)} %get-tuple-element.37), kind=kOutput, calls=%fused_computation.24 | convolution fusion | flops 1073741824 | bytes 6291456 | tf_op jit(solution)/shard_map/dot_general | solution.py:261
  138.5 4.1 %multiply_reduce_fusion = (f32[1024]{0:T(1024)S(1)}, f32[1024]{0:T(1024)S(1)}) fusion(bf16[4,4,2,64,1024]{4,3,2,1,0:T(8,128)(2,1)} %collective-permute-done.19, pred[64]{0:T(512)(128)(4,1)S(1)} %iota_compare_fusion.1, bf16[1,4,2,64,1024]{4,3,2,1,0:T(8,128)(2,1)S(1)} %bitcast.51, bf16[1,4,2,64,1024]{4,3,2,1,0:T(8,128)(2,1)S(1)} %bitcast.49, ...), kind=kLoop, calls=%fused_computation | loop fusion | flops 23066624 | bytes 8396864 | tf_op jit(solution)/shard_map/reduce_sum | solution.py:258
  143.5 4.5 %add_subtract_fusion = f32[256,1024]{1,0:T(8,128)} fusion(f32[256,1024]{1,0:T(8,128)S(1)} %fusion.37, bf16[2048,1024]{1,0:T(8,128)(2,1)} %bitcast.19, bf16[4096,256]{1,0:T(8,128)(2,1)S(1)} %copy-done.5, f32[1024]{0:T(1024)S(1)} %add.309, f32[256]{0:T(256)S(1)} %bitcast.61), kind=kOutput, calls=%fused_computation.26 | convolution fusion | flops 1074790400 | bytes 7345152 | tf_op jit(solution)/shard_map/dot_general | solution.py:261
  147.9 6.5 %all-to-all-done.cols_ref = bf16[64,56,256]{2,1,0:T(8,128)(2,1)} async-done(((bf16[64,56,256]{2,1,0:T(8,128)(2,1)}), bf16[64,56,256]{2,1,0:T(8,128)(2,1)}, u32[]{:S(2)}, u32[]{:S(2)}) %all-to-all-start) | async-done | bytes 1835040 | tf_op jit(solution)/shard_map/all_to_all | solution.py:248
  154.4 8.2 %new_state.1 = (f32[56,1024]{1,0:T(8,128)}, f32[1,1024]{1,0:T(1,128)}, bf16[56,1024]{1,0:T(8,128)(2,1)}) custom-call(s32[1]{0:T(128)} %bitcast.22.first_ref, s32[64]{0:T(128)} %get-tuple-element.65.entries_ref, bf16[64,8,512]{2,1,0:T(8,128)(2,1)} %pad_maximum_fusion.2.codes_ref, bf16[64,56,256]{2,1,0:T(8,128)(2,1)} %all-to-all-done.cols_ref, ...), custom_call_target="tpu_custom_call" | custom-call | flops 1879048192 | bytes 1835008 | tf_op jit(solution)/shard_map/new_state/pallas_call | solution.py:168
  (76 shorter events, 28.6 us)
Async XLA Ops:
  4.5 28.6 %collective-permute-start = (f16[128,896]{0,1:T(8,128)(2,1)}, f16[128,896]{0,1:T(8,128)(2,1)S(1)}, u32[]{:S(2)}, u32[]{:S(2)}) collective-permute-start(f16[128,896]{0,1:T(8,128)(2,1)} %get-tuple-element.55), channel_id=1, source_target_pairs={{0,1},{1,2},{2,3},{3,0},{4,5},{5,6},{6,7},{7,4},{8,9},{9,10},{10,1... | collective-permute-start | bytes 688136 | tf_op jit(solution)/shard_map/ppermute | solution.py:18
  8.4 25.2 %collective-permute-start.1 = (f16[128,896]{0,1:T(8,128)(2,1)S(1)}, f16[128,896]{0,1:T(8,128)(2,1)}, u32[]{:S(2)}, u32[]{:S(2)}) collective-permute-start(f16[128,896]{0,1:T(8,128)(2,1)S(1)} %get-tuple-element.54), channel_id=1, source_target_pairs={{0,3},{1,0},{2,1},{3,2},{4,7},{5,4},{6,5},{7,6},{8,11},{9,8},{10,9... | collective-permute-start | bytes 688136 | tf_op jit(solution)/shard_map/ppermute | solution.py:18
  13.1 17.2 %collective-permute-start.12 = (bf16[64,1024]{1,0:T(8,128)(2,1)S(1)}, bf16[64,1024]{1,0:T(8,128)(2,1)S(1)}, u32[]{:S(2)}, u32[]{:S(2)}) collective-permute-start(bf16[64,1024]{1,0:T(8,128)(2,1)S(1)} %fusion.64), channel_id=1, source_target_pairs={{0,32},{4,36},{8,40},{12,44},{16,48},{20,52},{24,56},{28,60},{32,0... | collective-permute-start | bytes 393224 | tf_op jit(solution)/shard_map/ppermute | solution.py:42
  16.8 34.4 %collective-permute-start.3 = (f16[128,896]{0,1:T(8,128)(2,1)}, f16[128,896]{0,1:T(8,128)(2,1)S(1)}, u32[]{:S(2)}, u32[]{:S(2)}) collective-permute-start(f16[128,896]{0,1:T(8,128)(2,1)} %slice_convert_fusion), channel_id=1, source_target_pairs={{0,3},{1,0},{2,1},{3,2},{4,7},{5,4},{6,5},{7,6},{8,11},{9,8},{10,9... | collective-permute-start | bytes 688136 | tf_op jit(solution)/shard_map/ppermute | solution.py:18
  22.0 29.8 %collective-permute-start.4 = (f16[128,896]{0,1:T(8,128)(2,1)}, f16[128,896]{0,1:T(8,128)(2,1)S(1)}, u32[]{:S(2)}, u32[]{:S(2)}) collective-permute-start(f16[128,896]{0,1:T(8,128)(2,1)} %slice_convert_fusion.1), channel_id=1, source_target_pairs={{0,1},{1,2},{2,3},{3,0},{4,5},{5,6},{6,7},{7,4},{8,9},{9,10},{10,1... | collective-permute-start | bytes 688136 | tf_op jit(solution)/shard_map/ppermute | solution.py:18
  30.4 8.0 %collective-permute-start.13 = (bf16[2,64,1024]{2,1,0:T(8,128)(2,1)S(1)}, bf16[2,64,1024]{2,1,0:T(8,128)(2,1)S(1)}, u32[]{:S(2)}, u32[]{:S(2)}) collective-permute-start(bf16[2,64,1024]{2,1,0:T(8,128)(2,1)S(1)} %pad_maximum_fusion.3), channel_id=1, source_target_pairs={{0,24},{4,28},{8,0},{12,4},{16,8},{20,12},{24,16},{28,20},{32,56},... | collective-permute-start | bytes 786440 | tf_op jit(solution)/shard_map/ppermute | solution.py:42
  33.2 7.8 %collective-permute-start.14 = (bf16[2,64,1024]{2,1,0:T(8,128)(2,1)S(1)}, bf16[2,64,1024]{2,1,0:T(8,128)(2,1)S(1)}, u32[]{:S(2)}, u32[]{:S(2)}) collective-permute-start(bf16[2,64,1024]{2,1,0:T(8,128)(2,1)S(1)} %pad_maximum_fusion.3), channel_id=1, source_target_pairs={{0,16},{4,20},{8,24},{12,28},{16,0},{20,4},{24,8},{28,12},{32,48},... | collective-permute-start | bytes 786440 | tf_op jit(solution)/shard_map/ppermute | solution.py:42
  33.5 15.0 %collective-permute-start.15 = (bf16[2,64,1024]{2,1,0:T(8,128)(2,1)S(1)}, bf16[2,64,1024]{2,1,0:T(8,128)(2,1)S(1)}, u32[]{:S(2)}, u32[]{:S(2)}) collective-permute-start(bf16[2,64,1024]{2,1,0:T(8,128)(2,1)S(1)} %pad_maximum_fusion.3), channel_id=1, source_target_pairs={{0,8},{4,12},{8,16},{12,20},{16,24},{20,28},{24,0},{28,4},{32,40},... | collective-permute-start | bytes 786440 | tf_op jit(solution)/shard_map/ppermute | solution.py:42
  38.3 14.0 %collective-permute-start.5 = (f16[128,896]{0,1:T(8,128)(2,1)S(1)}, f16[128,896]{0,1:T(8,128)(2,1)S(1)}, u32[]{:S(2)}, u32[]{:S(2)}) collective-permute-start(f16[128,896]{0,1:T(8,128)(2,1)S(1)} %fusion.57), channel_id=1, source_target_pairs={{0,3},{1,0},{2,1},{3,2},{4,7},{5,4},{6,5},{7,6},{8,11},{9,8},{10,9... | collective-permute-start | bytes 688136 | tf_op jit(solution)/shard_map/ppermute | solution.py:18
  40.9 11.4 %collective-permute-start.2 = (f16[128,896]{0,1:T(8,128)(2,1)S(1)}, f16[128,896]{0,1:T(8,128)(2,1)S(1)}, u32[]{:S(2)}, u32[]{:S(2)}) collective-permute-start(f16[128,896]{0,1:T(8,128)(2,1)S(1)} %fusion.60), channel_id=1, source_target_pairs={{0,1},{1,2},{2,3},{3,0},{4,5},{5,6},{6,7},{7,4},{8,9},{9,10},{10,1... | collective-permute-start | bytes 688136 | tf_op jit(solution)/shard_map/ppermute | solution.py:18
  48.7 27.2 %collective-permute-start.16 = (bf16[4,2,64,1024]{3,2,1,0:T(8,128)(2,1)S(1)}, bf16[4,2,64,1024]{3,2,1,0:T(8,128)(2,1)S(1)}, u32[]{:S(2)}, u32[]{:S(2)}) collective-permute-start(bf16[4,2,64,1024]{3,2,1,0:T(8,128)(2,1)S(1)} %pad_maximum_fusion.1), channel_id=1, source_target_pairs={{0,192},{4,196},{8,200},{12,204},{16,208},{20,212},{24,216},{28,22... | collective-permute-start | bytes 3145736 | tf_op jit(solution)/shard_map/ppermute | solution.py:42
  51.2 25.5 %collective-permute-start.17 = (bf16[4,2,64,1024]{3,2,1,0:T(8,128)(2,1)S(1)}, bf16[4,2,64,1024]{3,2,1,0:T(8,128)(2,1)S(1)}, u32[]{:S(2)}, u32[]{:S(2)}) collective-permute-start(bf16[4,2,64,1024]{3,2,1,0:T(8,128)(2,1)S(1)} %pad_maximum_fusion.1), channel_id=1, source_target_pairs={{0,128},{4,132},{8,136},{12,140},{16,144},{20,148},{24,152},{28,15... | collective-permute-start | bytes 3145736 | tf_op jit(solution)/shard_map/ppermute | solution.py:42
  51.8 48.5 %collective-permute-start.18 = (bf16[4,2,64,1024]{3,2,1,0:T(8,128)(2,1)S(1)}, bf16[4,2,64,1024]{3,2,1,0:T(8,128)(2,1)S(1)}, u32[]{:S(2)}, u32[]{:S(2)}) collective-permute-start(bf16[4,2,64,1024]{3,2,1,0:T(8,128)(2,1)S(1)} %pad_maximum_fusion.1), channel_id=1, source_target_pairs={{0,64},{4,68},{8,72},{12,76},{16,80},{20,84},{24,88},{28,92},{32,9... | collective-permute-start | bytes 3145736 | tf_op jit(solution)/shard_map/ppermute | solution.py:42
  52.8 10.5 %collective-permute-start.11 = (f16[448,256]{1,0:T(8,128)(2,1)S(1)}, f16[448,256]{1,0:T(8,128)(2,1)S(1)}, u32[]{:S(2)}, u32[]{:S(2)}) collective-permute-start(f16[448,256]{1,0:T(8,128)(2,1)S(1)} %get-tuple-element.53), channel_id=1, source_target_pairs={{0,1},{1,2},{2,3},{3,0},{4,5},{5,6},{6,7},{7,4},{8,9},{9,10},{10,1... | collective-permute-start | bytes 688136 | tf_op jit(solution)/shard_map/ppermute | solution.py:18
  52.9 10.7 %collective-permute-start.6 = (f16[448,256]{1,0:T(8,128)(2,1)S(1)}, f16[448,256]{1,0:T(8,128)(2,1)S(1)}, u32[]{:S(2)}, u32[]{:S(2)}) collective-permute-start(f16[448,256]{1,0:T(8,128)(2,1)S(1)} %get-tuple-element.52), channel_id=1, source_target_pairs={{0,3},{1,0},{2,1},{3,2},{4,7},{5,4},{6,5},{7,6},{8,11},{9,8},{10,9... | collective-permute-start | bytes 688136 | tf_op jit(solution)/shard_map/ppermute | solution.py:18
  63.3 12.6 %collective-permute-start.7 = (f16[448,256]{1,0:T(8,128)(2,1)S(1)}, f16[448,256]{1,0:T(8,128)(2,1)S(1)}, u32[]{:S(2)}, u32[]{:S(2)}) collective-permute-start(f16[448,256]{1,0:T(8,128)(2,1)S(1)} %get-tuple-element.53), channel_id=1, source_target_pairs={{0,3},{1,0},{2,1},{3,2},{4,7},{5,4},{6,5},{7,6},{8,11},{9,8},{10,9... | collective-permute-start | bytes 688136 | tf_op jit(solution)/shard_map/ppermute | solution.py:18
  63.6 12.3 %collective-permute-start.8 = (f16[448,256]{1,0:T(8,128)(2,1)S(1)}, f16[448,256]{1,0:T(8,128)(2,1)S(1)}, u32[]{:S(2)}, u32[]{:S(2)}) collective-permute-start(f16[448,256]{1,0:T(8,128)(2,1)S(1)} %get-tuple-element.52), channel_id=1, source_target_pairs={{0,1},{1,2},{2,3},{3,0},{4,5},{5,6},{6,7},{7,4},{8,9},{9,10},{10,1... | collective-permute-start | bytes 688136 | tf_op jit(solution)/shard_map/ppermute | solution.py:18
  76.7 25.9 %copy-start.1 = (bf16[4,2,64,1024]{3,2,1,0:T(8,128)(2,1)}, bf16[4,2,64,1024]{3,2,1,0:T(8,128)(2,1)S(1)}, u32[]{:S(2)}) copy-start(bf16[4,2,64,1024]{3,2,1,0:T(8,128)(2,1)S(1)} %collective-permute-done.17) | copy-start | bytes 3145732
  102.7 34.8 %collective-permute-start.19 = (bf16[4,4,2,64,1024]{4,3,2,1,0:T(8,128)(2,1)}, bf16[4,4,2,64,1024]{4,3,2,1,0:T(8,128)(2,1)}, u32[]{:S(2)}, u32[]{:S(2)}) collective-permute-start(bf16[4,4,2,64,1024]{4,3,2,1,0:T(8,128)(2,1)} %pad_maximum_fusion), channel_id=1, source_target_pairs={{0,4},{4,0},{8,12},{12,8},{16,20},{20,16},{24,28},{28,24},{32,36},... | collective-permute-start | bytes 12582920 | tf_op jit(solution)/shard_map/ppermute | solution.py:42
  103.8 13.2 %collective-permute-start.9 = (f16[448,256]{1,0:T(8,128)(2,1)S(1)}, f16[448,256]{1,0:T(8,128)(2,1)S(1)}, u32[]{:S(2)}, u32[]{:S(2)}) collective-permute-start(f16[448,256]{1,0:T(8,128)(2,1)S(1)} %collective-permute-done.8), channel_id=1, source_target_pairs={{0,1},{1,2},{2,3},{3,0},{4,5},{5,6},{6,7},{7,4},{8,9},{9,10},{10,1... | collective-permute-start | bytes 688136 | tf_op jit(solution)/shard_map/ppermute | solution.py:18
  103.9 13.9 %collective-permute-start.10 = (f16[448,256]{1,0:T(8,128)(2,1)S(1)}, f16[448,256]{1,0:T(8,128)(2,1)S(1)}, u32[]{:S(2)}, u32[]{:S(2)}) collective-permute-start(f16[448,256]{1,0:T(8,128)(2,1)S(1)} %collective-permute-done.7), channel_id=1, source_target_pairs={{0,3},{1,0},{2,1},{3,2},{4,7},{5,4},{6,5},{7,6},{8,11},{9,8},{10,9... | collective-permute-start | bytes 688136 | tf_op jit(solution)/shard_map/ppermute | solution.py:18
  122.8 31.6 %all-to-all-start = ((bf16[64,56,256]{2,1,0:T(8,128)(2,1)}), bf16[64,56,256]{2,1,0:T(8,128)(2,1)}, u32[]{:S(2)}, u32[]{:S(2)}) async-start(bf16[64,56,256]{2,1,0:T(8,128)(2,1)} %bitcast.43), calls=%async_computation | async-start | bytes 3670016 | tf_op jit(solution)/shard_map/all_to_all | solution.py:248
  132.6 5.9 %copy-start.2 = (bf16[4,2,64,1024]{3,2,1,0:T(8,128)(2,1)S(1)}, bf16[4,2,64,1024]{3,2,1,0:T(8,128)(2,1)}, u32[]{:S(2)}) copy-start(bf16[4,2,64,1024]{3,2,1,0:T(8,128)(2,1)} %copy-done.1) | copy-start | bytes 3145732
  132.6 5.9 %copy-start.4 = (bf16[4,2,64,1024]{3,2,1,0:T(8,128)(2,1)S(1)}, bf16[4,2,64,1024]{3,2,1,0:T(8,128)(2,1)}, u32[]{:S(2)}) copy-start(bf16[4,2,64,1024]{3,2,1,0:T(8,128)(2,1)} %copy-done.3) | copy-start | bytes 3145732
  (4 other events, 13.4 us)
where the time goes:
time: 163 us
  waiting for transfers between devices  74.8 us (46%)
  starting transfers between devices  35.6 us (22%)
  matrix products  16.7 us (10%)
  Pallas kernels  15.5 us (10%)
  other arithmetic  15.1 us (9%)
  local copies, waits for them, and re-layouts  4 us (2%)
    ppermute x8, waiting for transfers between devices, dp_shift(): return lax.ppermute(value, 'dp', pairs)  41.3 us
    ppermute x12, waiting for transfers between devices, mp_shift(): return lax.ppermute(value, 'mp', [(i, (i + step) % MP) for i in range(MP)])  27 us
    ppermute x12, starting transfers between devices, mp_shift(): return lax.ppermute(value, 'mp', [(i, (i + step) % MP) for i in range(MP)])  21.5 us
    ppermute x8, starting transfers between devices, dp_shift(): return lax.ppermute(value, 'dp', pairs)  8.85 us
    dot_general x4, matrix products, partial(): return jnp.dot(pooled, w, preferred_element_type=jnp.float32) * SCALE  8.41 us
    dot_general x2, matrix products, step(): lax.dot_general(part, rows, (((0,), (0,)), ((), ())), preferred_element_t...  8.25 us
    pallas_call x1, Pallas kernels, new_state(): pl.pallas_call(sums_kernel, grid_spec=pltpu.PrefetchScalarGridSpec(num_sc...  8.16 us
    all_to_all x1, waiting for transfers between devices, step(): lax.all_to_all(embedded.reshape(shards, feature_cols, docs), 'dp', split_...  6.48 us
  transfers between devices with their start and end apart: 21, of which 10 were waited for; matrix products, arithmetic and copies ran while one was open for 18% of the time, Pallas kernels for 4%

commit v1 on v0

--- a/solution.py
+++ b/solution.py
@@ -42,64 +42,90 @@
     return lax.ppermute(value, "dp", pairs)
 
 
-def gather_line(piece, hold):
+def shifts(value, dim):
+    return [value] + [dp_shift(value, dim, -step) for step in (1, 2, 3)]
+
+
+def first_lines(piece, hold):
+    half = piece.shape[0] // 2
     pair = jnp.stack([piece, after(dp_shift(piece, 1, 1), hold)])
-    return [pair] + [dp_shift(pair, 2, -step) for step in (1, 2, 3)]
-
-
-def gather_plane(line, hold):
-    line = jnp.stack(after(line, hold))
-    return [line] + [dp_shift(line, 0, -step) for step in (1, 2, 3)]
-
-
-def gather_table(plane, hold):
-    plane = jnp.stack(after(plane, hold))
-    return plane, dp_shift(plane, 3, 1)
+    return shifts(pair[:, :half], 2), shifts(pair[:, half:], 0)
+
+
+def second_lines(upper, lower, hold):
+    upper, lower = after((upper, lower), hold)
+    return shifts(jnp.stack(upper), 0), shifts(jnp.stack(lower), 2)
+
+
+def gather_tables(upper, lower, hold):
+    upper, lower = after((upper, lower), hold)
+    tables = [jnp.stack(upper), jnp.stack(lower)]
+    return tables + [dp_shift(t, 3, 1) for t in tables]
 
 
 def table_order(index):
     my = (index // 16, index // 8 % 2, index // 2 % 4, index % 2)
     i = jnp.arange(64, dtype=jnp.int32)
-    x, low, y, core = (my[0] + i // 8) % 4, (my[1] + i) % 2, (my[2] + i // 2) % 4, (my[3] + i // 32) % 2
-    blocks = ((x * 2 + low) * 4 + y) * 2 + core
+
+    def block(x, y):
+        low, core = (my[1] + i) % 2, (my[3] + i // 32) % 2
+        return (((my[0] + x) % 4 * 2 + low) * 4 + (my[2] + y) % 4) * 2 + core
+
+    upper, lower = block(i // 8, i // 2), block(i // 2, i // 8)
     x, low, y, core = (i // 16 - my[0]) % 4, (i // 8 - my[1]) % 2, (i // 2 - my[2]) % 4, (i - my[3]) % 2
-    entries = ((core * 4 + x) * 4 + y) * 2 + low
-    return blocks.astype(jnp.int32), entries.astype(jnp.int32)
+    entries = ((core * 4 + y) * 4 + x) * 2 + low
+    return jnp.concatenate([upper, lower]).astype(jnp.int32), entries.astype(jnp.int32)
 
 
 def place_kernel(at_ref, *refs):
-    pieces, out_ref = refs[:-1], refs[-1]
+    pieces, out_ref, sems = refs[:-2], refs[-2], refs[-1]
     rows = pieces[0].shape[0]
-    for i, piece in enumerate(pieces):
-        out_ref[pl.ds(pl.multiple_of(at_ref[i], 64), rows), :] = piece[...]
+    copies = [
+        pltpu.make_async_copy(piece, out_ref.at[pl.ds(pl.multiple_of(at_ref[i], 64), rows)], sems.at[i])
+        for i, piece in enumerate(pieces)
+    ]
+    for copy in copies:
+        copy.start()
+    for copy in copies:
+        copy.wait()
 
 
 def put_in_place(at, pieces):
     rows, docs = pieces[0].shape
     total = rows * len(pieces)
-    whole = pl.BlockSpec(memory_space=pltpu.VMEM)
     return pl.pallas_call(
         place_kernel,
         grid_spec=pltpu.PrefetchScalarGridSpec(
-            num_scalar_prefetch=1, grid=(), in_specs=[whole] * len(pieces), out_specs=whole
+            num_scalar_prefetch=1,
+            grid=(),
+            in_specs=[pl.BlockSpec(memory_space=pltpu.VMEM)] * len(pieces),
+            out_specs=pl.BlockSpec(memory_space=pl.ANY),
+            scratch_shapes=[pltpu.SemaphoreType.DMA((len(pieces),))],
         ),
         out_shape=jax.ShapeDtypeStruct((total, docs), jnp.bfloat16),
         cost_estimate=pl.CostEstimate(flops=1_000_000, bytes_accessed=4 * total * docs, transcendentals=0),
+        compiler_params=pltpu.CompilerParams(vmem_limit_bytes=4 * 1024 * 1024),
         name="put_in_place",
     )(at, *pieces)
 
 
 def order_kernel(blocks_ref, whole_ref, order_ref, norms_ref):
     docs = whole_ref.shape[1]
-    cols, tall = whole_ref.shape[0] // 64, order_ref.shape[0] // 64
-    zeros = jnp.zeros((tall - cols, docs), jnp.bfloat16)
+    cols = whole_ref.shape[0] // 64
+    upper = order_ref.shape[0] // 128
+    zeros = jnp.zeros((2 * upper - cols, docs), jnp.bfloat16)
     norms = jnp.zeros((8, docs), jnp.float32)
-    for i in range(64):
-        block = whole_ref[pl.ds(pl.multiple_of(blocks_ref[i] * cols, 8), cols), :]
-        wide = block.astype(jnp.float32)
-        norms += jnp.sum((wide * wide).reshape(cols // 8, 8, docs), axis=0)
-        order_ref[i * tall : i * tall + cols, :] = block
-        order_ref[i * tall + cols : (i + 1) * tall, :] = zeros
+    for part in range(4):
+        rows, first = (upper, 0) if part % 2 == 0 else (cols - upper, upper)
+        for i in range(32):
+            block = blocks_ref[part % 2 * 64 + part // 2 * 32 + i]
+            block = whole_ref[pl.ds(pl.multiple_of(block * cols + first, 8), rows), :]
+            wide = block.astype(jnp.float32)
+            norms += jnp.sum((wide * wide).reshape(rows // 8, 8, docs), axis=0)
+            to = (part * 32 + i) * upper
+            order_ref[to : to + rows, :] = block
+            if rows < upper:
+                order_ref[to + rows : to + upper, :] = zeros
     norms_ref[...] = jnp.sum(norms, axis=0, keepdims=True)
 
 
@@ -212,17 +238,17 @@
     centers = (sums_t / ema_counts[None, :]).astype(jnp.bfloat16)
     pair = jnp.stack([assignments // 64, assignments % 64]).astype(jnp.bfloat16).reshape(1, 2 * docs)
     extra = jnp.pad(pair, ((0, 7), (0, width - 2 * docs)))
-    centers = after(jnp.concatenate([centers, extra]), far)
+    centers = jnp.concatenate([centers, extra])
     ahead, behind = partial(1), partial(-1)
     low_a, top_b = ahead[half_docs:].astype(f16), behind[:half_docs].astype(f16)
-    line = gather_line(centers, (low_a, top_b))
+    lines = first_lines(centers, (low_a, top_b))
     near = (low_a, top_b)
     low_a, top_b = mp_shift(low_a, 1), mp_shift(top_b, -1)
     mine = partial(0)
     up, down = after((up, down), near, mine)
     top_a = (ahead[:half_docs] + up.astype(jnp.float32)).astype(f16)
     low_b = (behind[half_docs:] + down.astype(jnp.float32)).astype(f16)
-    plane = gather_plane(line, (top_a, low_b))
+    lines = second_lines(*lines, (top_a, low_b))
     top_a, low_b = mp_shift(top_a, 1), mp_shift(low_b, -1)
     top = mine[:half_docs] + top_a.astype(jnp.float32) + top_b.astype(jnp.float32)
     low = mine[half_docs:] + low_a.astype(jnp.float32) + low_b.astype(jnp.float32)
@@ -235,7 +261,7 @@
     c_first = mp_shift(a_first, 1)
     c_second = mp_shift(b_second, -1)
 
-    tables = gather_table(plane, (a_first, b_second, a_second, b_first))
+    tables = gather_tables(*lines, (a_first, b_second, a_second, b_first))
     blocks, entries = table_order(index)
     parts = [first_half, second_half, b_first, b_second, c_first, c_second, a_first, a_second]
     i = jnp.arange(len(parts), dtype=jnp.int32)
@@ -249,12 +275,15 @@
         embedded.reshape(shards, feature_cols, docs), "dp", split_axis=0, concat_axis=0, tiled=True
     )
     ordered, doc_norms = put_in_order(blocks, embedded)
-    tables = [t.reshape(shards // 2, feature_cols + 8, width) for t in tables]
-    codes = jnp.concatenate([t[:, feature_cols:, : 2 * docs] for t in tables])
-    real = lax.broadcasted_iota(jnp.int32, tables[0].shape, 1) < feature_cols
+    upper = (feature_cols + 8) // 2
+    tables = [t.reshape(shards // 2, upper, width) for t in tables]
+    real = feature_cols - upper
+    codes = jnp.concatenate([t[:, real:, : 2 * docs] for t in tables[1::2]])
     center_norms, products = 0.0, 0.0
     for i, table in enumerate(tables):
-        wide = jnp.where(real, table.astype(jnp.float32), 0.0)
+        wide = table.astype(jnp.float32)
+        if i % 2:
+            wide = jnp.where(lax.broadcasted_iota(jnp.int32, table.shape, 1) < real, wide, 0.0)
         center_norms = center_norms + jnp.sum(wide * wide, axis=(0, 1))
         rows = table.reshape(-1, width)
         part = ordered[i * rows.shape[0] : (i + 1) * rows.shape[0]]

time: 163 us -> 155 us (0.951)
  waiting for transfers between devices: 74.8 us -> 55.5 us
  starting transfers between devices: 35.6 us -> 51.3 us
  local copies, waits for them, and re-layouts: 4 us -> 1.24 us
  Pallas kernels: 15.5 us -> 13.8 us
    ppermute x8 -> x15, waiting for transfers between devices: 41.3 us -> 17.4 us  [dp_shift(): return lax.ppermute(value, 'dp', pairs)]
    ppermute x8 -> x15, starting transfers between devices: 8.85 us -> 20.2 us  [dp_shift(): return lax.ppermute(value, 'dp', pairs)]
    ppermute x12, waiting for transfers between devices: 27 us -> 31.4 us  [mp_shift(): return lax.ppermute(value, 'mp', [(i, (i + step) % MP) for i in range(MP)])]
    all_to_all x1, starting transfers between devices: 5.32 us -> 8.39 us  [step(): lax.all_to_all(embedded.reshape(shards, feature_cols, docs), 'dp', split_...]
    pallas_call x1, Pallas kernels: 3.55 us -> 1.84 us  [put_in_place(): pl.pallas_call(place_kernel, grid_spec=pltpu.PrefetchScalarGridSpec(num_s...]
    reduce_sum x1 -> x3, other arithmetic: 4.1 us -> 5.34 us  [step(): center_norms = center_norms + jnp.sum(wide * wide, axis=(0, 1))]
    dot_general x2 -> x4, matrix products: 8.25 us -> 9.02 us  [step(): lax.dot_general(part, rows, (((0,), (0,)), ((), ())), preferred_element_t...]
    another operation x7 -> x8, other arithmetic: 4.85 us -> 4.37 us  [the longest x1 2.38 us: gather_table(): plane = jnp.stack(after(plane, hold))]
  transfers between devices with their start and end apart: 21 -> 28, of which waited for: 10 -> 13; matrix products, arithmetic and copies ran while one was open for 18% -> 20% of each run, Pallas kernels for 4% -> 4%
where the time goes in v1:
time: 155 us; the launch traced here: 154 us
  waiting for transfers between devices  55.5 us (36%)
  starting transfers between devices  51.3 us (33%)
  matrix products  17.4 us (11%)
  other arithmetic  14.1 us (9%)
  Pallas kernels  13.8 us (9%)
    ppermute x12, waiting for transfers between devices, mp_shift(): return lax.ppermute(value, 'mp', [(i, (i + step) % MP) for i in range(MP)])  31.4 us
    ppermute x12, starting transfers between devices, mp_shift(): return lax.ppermute(value, 'mp', [(i, (i + step) % MP) for i in range(MP)])  22.7 us
    ppermute x15, starting transfers between devices, dp_shift(): return lax.ppermute(value, 'dp', pairs)  20.2 us
    ppermute x15, waiting for transfers between devices, dp_shift(): return lax.ppermute(value, 'dp', pairs)  17.4 us
    dot_general x4, matrix products, step(): lax.dot_general(part, rows, (((0,), (0,)), ((), ())), preferred_element_t...  9.02 us
    dot_general x4, matrix products, partial(): return jnp.dot(pooled, w, preferred_element_type=jnp.float32) * SCALE  8.42 us
    all_to_all x1, starting transfers between devices, step(): lax.all_to_all(embedded.reshape(shards, feature_cols, docs), 'dp', split_...  8.39 us
    pallas_call x1, Pallas kernels, new_state(): pl.pallas_call(sums_kernel, grid_spec=pltpu.PrefetchScalarGridSpec(num_sc...  8.16 us
  transfers between devices with their start and end apart: 28, of which 13 were waited for; matrix products, arithmetic and copies ran while one was open for 20% of the time, Pallas kernels for 4%

profile of v1, /device:TPU:1, one launch (start us, length us, event | category | flops | bytes accessed | tf_op | source)
XLA Modules:
  0.0 154.4 jit_solution(7732342462154782933)
XLA Ops:
  2.4 2.5 %collective-permute-start.12 = (bf16[64,1024]{1,0:T(8,128)(2,1)S(1)}, bf16[64,1024]{1,0:T(8,128)(2,1)}, u32[]{:S(2)}, u32[]{:S(2)}) collective-permute-start(bf16[64,1024]{1,0:T(8,128)(2,1)S(1)} %get-tuple-element.74), channel_id=1, source_target_pairs={{0,32},{4,36},{8,40},{12,44},{16,48},{20,52},{24,56},{28,60},{32,0... | collective-permute-start | bytes 393224 | tf_op jit(solution)/shard_map/ppermute | solution.py:42
  7.2 5.2 %collective-permute-start.1 = (f16[128,896]{0,1:T(8,128)(2,1)S(1)}, f16[128,896]{0,1:T(8,128)(2,1)S(1)}, u32[]{:S(2)}, u32[]{:S(2)}) collective-permute-start(f16[128,896]{0,1:T(8,128)(2,1)S(1)} %get-tuple-element.70), channel_id=1, source_target_pairs={{0,3},{1,0},{2,1},{3,2},{4,7},{5,4},{6,5},{7,6},{8,11},{9,8},{10,9... | collective-permute-start | bytes 688136 | tf_op jit(solution)/shard_map/ppermute | solution.py:18
  17.3 2.1 %fusion.28 = f32[256,896]{0,1:T(8,128)S(1)} fusion(bf16[256,896]{1,0:T(8,128)(2,1)S(1)} %copy-done, bf16[896,3584]{1,0:T(8,128)(2,1)} %param.6, s32[]{:T(128)S(6)} %select_n.171), kind=kOutput, calls=%fused_computation.24 | convolution fusion | flops 411271168 | bytes 2981892 | tf_op jit(solution)/shard_map/dot_general | solution.py:232
  21.8 2.4 %collective-permute-start.17 = (bf16[2,32,1024]{2,1,0:T(8,128)(2,1)S(1)}, bf16[2,32,1024]{2,1,0:T(8,128)(2,1)S(1)}, u32[]{:S(2)}, u32[]{:S(2)}) collective-permute-start(bf16[2,32,1024]{2,1,0:T(8,128)(2,1)S(1)} %get-tuple-element.39), channel_id=1, source_target_pairs={{0,128},{4,132},{8,136},{12,140},{16,144},{20,148},{24,152},{28,15... | collective-permute-start | bytes 393224 | tf_op jit(solution)/shard_map/ppermute | solution.py:42
  26.7 2.6 %collective-permute-start.14 = (bf16[2,32,1024]{2,1,0:T(8,128)(2,1)S(1)}, bf16[2,32,1024]{2,1,0:T(8,128)(2,1)S(1)}, u32[]{:S(2)}, u32[]{:S(2)}) collective-permute-start(bf16[2,32,1024]{2,1,0:T(8,128)(2,1)S(1)} %get-tuple-element.35), channel_id=1, source_target_pairs={{0,16},{4,20},{8,24},{12,28},{16,0},{20,4},{24,8},{28,12},{32,48},... | collective-permute-start | bytes 393224 | tf_op jit(solution)/shard_map/ppermute | solution.py:42
  32.1 2.2 %collective-permute-start.3 = (f16[128,896]{0,1:T(8,128)(2,1)S(1)}, f16[128,896]{0,1:T(8,128)(2,1)S(1)}, u32[]{:S(2)}, u32[]{:S(2)}) collective-permute-start(f16[128,896]{0,1:T(8,128)(2,1)S(1)} %slice_convert_fusion), channel_id=1, source_target_pairs={{0,3},{1,0},{2,1},{3,2},{4,7},{5,4},{6,5},{7,6},{8,11},{9,8},{10,9... | collective-permute-start | bytes 688136 | tf_op jit(solution)/shard_map/ppermute | solution.py:18
  34.5 3.4 %collective-permute-start.5 = (f16[128,896]{0,1:T(8,128)(2,1)S(1)}, f16[128,896]{0,1:T(8,128)(2,1)S(1)}, u32[]{:S(2)}, u32[]{:S(2)}) collective-permute-start(f16[128,896]{0,1:T(8,128)(2,1)S(1)} %fusion.59), channel_id=1, source_target_pairs={{0,3},{1,0},{2,1},{3,2},{4,7},{5,4},{6,5},{7,6},{8,11},{9,8},{10,9... | collective-permute-start | bytes 688136 | tf_op jit(solution)/shard_map/ppermute | solution.py:18
  39.3 5.7 %collective-permute-done.3 = f16[128,896]{0,1:T(8,128)(2,1)S(1)} collective-permute-done((f16[128,896]{0,1:T(8,128)(2,1)S(1)}, f16[128,896]{0,1:T(8,128)(2,1)S(1)}, u32[]{:S(2)}, u32[]{:S(2)}) %collective-permute-start.3) | collective-permute-done | bytes 229408 | tf_op jit(solution)/shard_map/ppermute | solution.py:18
  47.1 7.0 %collective-permute-done.5 = f16[128,896]{0,1:T(8,128)(2,1)S(1)} collective-permute-done((f16[128,896]{0,1:T(8,128)(2,1)S(1)}, f16[128,896]{0,1:T(8,128)(2,1)S(1)}, u32[]{:S(2)}, u32[]{:S(2)}) %collective-permute-start.5) | collective-permute-done | bytes 229408 | tf_op jit(solution)/shard_map/ppermute | solution.py:18
  54.5 3.3 %collective-permute-start.6 = (f16[448,256]{1,0:T(8,128)(2,1)S(1)}, f16[448,256]{1,0:T(8,128)(2,1)S(1)}, u32[]{:S(2)}, u32[]{:S(2)}) collective-permute-start(f16[448,256]{1,0:T(8,128)(2,1)S(1)} %get-tuple-element.68), channel_id=1, source_target_pairs={{0,3},{1,0},{2,1},{3,2},{4,7},{5,4},{6,5},{7,6},{8,11},{9,8},{10,9... | collective-permute-start | bytes 688136 | tf_op jit(solution)/shard_map/ppermute | solution.py:18
  57.8 3.6 %collective-permute-start.7 = (f16[448,256]{1,0:T(8,128)(2,1)S(1)}, f16[448,256]{1,0:T(8,128)(2,1)S(1)}, u32[]{:S(2)}, u32[]{:S(2)}) collective-permute-start(f16[448,256]{1,0:T(8,128)(2,1)S(1)} %get-tuple-element.69), channel_id=1, source_target_pairs={{0,3},{1,0},{2,1},{3,2},{4,7},{5,4},{6,5},{7,6},{8,11},{9,8},{10,9... | collective-permute-start | bytes 688136 | tf_op jit(solution)/shard_map/ppermute | solution.py:18
  61.4 11.8 %collective-permute-done.6 = f16[448,256]{1,0:T(8,128)(2,1)S(1)} collective-permute-done((f16[448,256]{1,0:T(8,128)(2,1)S(1)}, f16[448,256]{1,0:T(8,128)(2,1)S(1)}, u32[]{:S(2)}, u32[]{:S(2)}) %collective-permute-start.6) | collective-permute-done | bytes 229408 | tf_op jit(solution)/shard_map/ppermute | solution.py:18
  80.1 2.7 %collective-permute-start.19 = (bf16[4,2,32,1024]{3,2,1,0:T(8,128)(2,1)S(1)}, bf16[4,2,32,1024]{3,2,1,0:T(8,128)(2,1)S(1)}, u32[]{:S(2)}, u32[]{:S(2)}) collective-permute-start(bf16[4,2,32,1024]{3,2,1,0:T(8,128)(2,1)S(1)} %pad_maximum_fusion.2), channel_id=1, source_target_pairs={{0,192},{4,196},{8,200},{12,204},{16,208},{20,212},{24,216},{28,22... | collective-permute-start | bytes 1572872 | tf_op jit(solution)/shard_map/ppermute | solution.py:42
  83.3 4.3 %collective-permute-done.23 = bf16[4,2,32,1024]{3,2,1,0:T(8,128)(2,1)S(1)} collective-permute-done((bf16[4,2,32,1024]{3,2,1,0:T(8,128)(2,1)S(1)}, bf16[4,2,32,1024]{3,2,1,0:T(8,128)(2,1)S(1)}, u32[]{:S(2)}, u32[]{:S(2)}) %collective-permute-start.23) | collective-permute-done | bytes 524320 | tf_op jit(solution)/shard_map/ppermute | solution.py:42
  88.7 8.9 %collective-permute-done.22 = bf16[4,2,32,1024]{3,2,1,0:T(8,128)(2,1)S(1)} collective-permute-done((bf16[4,2,32,1024]{3,2,1,0:T(8,128)(2,1)S(1)}, bf16[4,2,32,1024]{3,2,1,0:T(8,128)(2,1)S(1)}, u32[]{:S(2)}, u32[]{:S(2)}) %collective-permute-start.22) | collective-permute-done | bytes 524320 | tf_op jit(solution)/shard_map/ppermute | solution.py:42
  97.7 2.2 %collective-permute-start.10 = (f16[448,256]{1,0:T(8,128)(2,1)S(1)}, f16[448,256]{1,0:T(8,128)(2,1)S(1)}, u32[]{:S(2)}, u32[]{:S(2)}) collective-permute-start(f16[448,256]{1,0:T(8,128)(2,1)S(1)} %collective-permute-done.7), channel_id=1, source_target_pairs={{0,3},{1,0},{2,1},{3,2},{4,7},{5,4},{6,5},{7,6},{8,11},{9,8},{10,9... | collective-permute-start | bytes 688136 | tf_op jit(solution)/shard_map/ppermute | solution.py:18
  99.9 3.7 %collective-permute-done.21 = bf16[4,2,32,1024]{3,2,1,0:T(8,128)(2,1)S(1)} collective-permute-done((bf16[4,2,32,1024]{3,2,1,0:T(8,128)(2,1)S(1)}, bf16[4,2,32,1024]{3,2,1,0:T(8,128)(2,1)S(1)}, u32[]{:S(2)}, u32[]{:S(2)}) %collective-permute-start.21) | collective-permute-done | bytes 524320 | tf_op jit(solution)/shard_map/ppermute | solution.py:42
  111.7 8.4 %all-to-all-start = ((bf16[64,56,256]{2,1,0:T(8,128)(2,1)}), bf16[64,56,256]{2,1,0:T(8,128)(2,1)}, u32[]{:S(2)}, u32[]{:S(2)}) async-start(bf16[64,56,256]{2,1,0:T(8,128)(2,1)} %bitcast.5), calls=%async_computation | async-start | bytes 3670016 | tf_op jit(solution)/shard_map/all_to_all | solution.py:274
  122.3 3.8 %put_in_order.1 = (bf16[4096,256]{1,0:T(8,128)(2,1)}, f32[1,256]{1,0:T(1,128)}) custom-call(s32[128]{0:T(128)} %pad_add_fusion.blocks_ref, bf16[3584,256]{1,0:T(8,128)(2,1)} %put_in_place.1.whole_ref), custom_call_target="tpu_custom_call" | custom-call | flops 3000000 | bytes 3670016 | tf_op jit(solution)/shard_map/put_in_order/pallas_call | solution.py:135
  126.1 2.6 %fusion.41 = f32[256,1024]{1,0:T(8,128)S(1)} fusion(bf16[1024,1024]{1,0:T(8,128)(2,1)} %bitcast.26, bf16[4096,256]{1,0:T(8,128)(2,1)} %get-tuple-element.51), kind=kOutput, calls=%fused_computation.51 | convolution fusion | flops 536870912 | bytes 3670016 | tf_op jit(solution)/shard_map/dot_general | solution.py:290
  128.8 2.3 %convolution_add_fusion.1 = f32[256,1024]{1,0:T(8,128)S(1)} fusion(f32[256,1024]{1,0:T(8,128)S(1)} %fusion.41, bf16[1024,1024]{1,0:T(8,128)(2,1)} %bitcast.27, bf16[4096,256]{1,0:T(8,128)(2,1)S(1)} %copy-done.1), kind=kOutput, calls=%fused_computation.17 | convolution fusion | flops 537133056 | bytes 4718592 | tf_op jit(solution)/shard_map/dot_general | solution.py:290
  136.2 3.4 %add_subtract_fusion = f32[256,1024]{1,0:T(8,128)} fusion(f32[256,1024]{1,0:T(8,128)S(1)} %fusion.37, f32[256,1024]{1,0:T(8,128)S(1)} %convolution_add_fusion.1, bf16[1024,1024]{1,0:T(8,128)(2,1)} %bitcast.28, bf16[4096,256]{1,0:T(8,128)(2,1)S(1)} %copy-done.1, f32[1024]{0:T(1024)S(1)} %add_add_fusion, f32[256]{0:T(256)S(1)} %bitcast.79), kind=kOutput, calls=%fused_computation.27 | convolution fusion | flops 538181632 | bytes 5772288 | tf_op jit(solution)/shard_map/dot_general | solution.py:290
  139.6 6.7 %all-to-all-done.cols_ref = bf16[64,56,256]{2,1,0:T(8,128)(2,1)} async-done(((bf16[64,56,256]{2,1,0:T(8,128)(2,1)}), bf16[64,56,256]{2,1,0:T(8,128)(2,1)}, u32[]{:S(2)}, u32[]{:S(2)}) %all-to-all-start) | async-done | bytes 1835040 | tf_op jit(solution)/shard_map/all_to_all | solution.py:274
  146.3 8.2 %new_state.1 = (f32[56,1024]{1,0:T(8,128)}, f32[1,1024]{1,0:T(1,128)}, bf16[56,1024]{1,0:T(8,128)(2,1)}) custom-call(s32[1]{0:T(128)} %bitcast.32.first_ref, s32[64]{0:T(128)} %fusion.80.entries_ref, bf16[64,8,512]{2,1,0:T(8,128)(2,1)} %pad_maximum_fusion.4.codes_ref, bf16[64,56,256]{2,1,0:T(8,128)(2,1)} %all-to-all-done.cols_ref, f32[56,1024]{1,0:T(8,128)} %bitcast.72, ...), custom_call_target="tpu_custom_call" | custom-call | flops 1879048192 | bytes 1835008 | tf_op jit(solution)/shard_map/new_state/pallas_call | solution.py:194
  (103 shorter events, 44.2 us)
Async XLA Ops:
  2.4 17.1 %collective-permute-start.12 = (bf16[64,1024]{1,0:T(8,128)(2,1)S(1)}, bf16[64,1024]{1,0:T(8,128)(2,1)}, u32[]{:S(2)}, u32[]{:S(2)}) collective-permute-start(bf16[64,1024]{1,0:T(8,128)(2,1)S(1)} %get-tuple-element.74), channel_id=1, source_target_pairs={{0,32},{4,36},{8,40},{12,44},{16,48},{20,52},{24,56},{28,60},{32,0... | collective-permute-start | bytes 393224 | tf_op jit(solution)/shard_map/ppermute | solution.py:42
  7.2 18.2 %collective-permute-start.1 = (f16[128,896]{0,1:T(8,128)(2,1)S(1)}, f16[128,896]{0,1:T(8,128)(2,1)S(1)}, u32[]{:S(2)}, u32[]{:S(2)}) collective-permute-start(f16[128,896]{0,1:T(8,128)(2,1)S(1)} %get-tuple-element.70), channel_id=1, source_target_pairs={{0,3},{1,0},{2,1},{3,2},{4,7},{5,4},{6,5},{7,6},{8,11},{9,8},{10,9... | collective-permute-start | bytes 688136 | tf_op jit(solution)/shard_map/ppermute | solution.py:18
  12.4 14.3 %collective-permute-start = (f16[128,896]{0,1:T(8,128)(2,1)S(1)}, f16[128,896]{0,1:T(8,128)(2,1)S(1)}, u32[]{:S(2)}, u32[]{:S(2)}) collective-permute-start(f16[128,896]{0,1:T(8,128)(2,1)S(1)} %get-tuple-element.71), channel_id=1, source_target_pairs={{0,1},{1,2},{2,3},{3,0},{4,5},{5,6},{6,7},{7,4},{8,9},{9,10},{10,1... | collective-permute-start | bytes 688136 | tf_op jit(solution)/shard_map/ppermute | solution.py:18
  20.5 8.9 %collective-permute-start.18 = (bf16[2,32,1024]{2,1,0:T(8,128)(2,1)S(1)}, bf16[2,32,1024]{2,1,0:T(8,128)(2,1)S(1)}, u32[]{:S(2)}, u32[]{:S(2)}) collective-permute-start(bf16[2,32,1024]{2,1,0:T(8,128)(2,1)S(1)} %get-tuple-element.39), channel_id=1, source_target_pairs={{0,64},{4,68},{8,72},{12,76},{16,80},{20,84},{24,88},{28,92},{32,9... | collective-permute-start | bytes 393224 | tf_op jit(solution)/shard_map/ppermute | solution.py:42
  21.8 8.8 %collective-permute-start.17 = (bf16[2,32,1024]{2,1,0:T(8,128)(2,1)S(1)}, bf16[2,32,1024]{2,1,0:T(8,128)(2,1)S(1)}, u32[]{:S(2)}, u32[]{:S(2)}) collective-permute-start(bf16[2,32,1024]{2,1,0:T(8,128)(2,1)S(1)} %get-tuple-element.39), channel_id=1, source_target_pairs={{0,128},{4,132},{8,136},{12,140},{16,144},{20,148},{24,152},{28,15... | collective-permute-start | bytes 393224 | tf_op jit(solution)/shard_map/ppermute | solution.py:42
  25.4 9.0 %collective-permute-start.15 = (bf16[2,32,1024]{2,1,0:T(8,128)(2,1)S(1)}, bf16[2,32,1024]{2,1,0:T(8,128)(2,1)S(1)}, u32[]{:S(2)}, u32[]{:S(2)}) collective-permute-start(bf16[2,32,1024]{2,1,0:T(8,128)(2,1)S(1)} %get-tuple-element.35), channel_id=1, source_target_pairs={{0,8},{4,12},{8,16},{12,20},{16,24},{20,28},{24,0},{28,4},{32,40},... | collective-permute-start | bytes 393224 | tf_op jit(solution)/shard_map/ppermute | solution.py:42
  32.1 12.9 %collective-permute-start.3 = (f16[128,896]{0,1:T(8,128)(2,1)S(1)}, f16[128,896]{0,1:T(8,128)(2,1)S(1)}, u32[]{:S(2)}, u32[]{:S(2)}) collective-permute-start(f16[128,896]{0,1:T(8,128)(2,1)S(1)} %slice_convert_fusion), channel_id=1, source_target_pairs={{0,3},{1,0},{2,1},{3,2},{4,7},{5,4},{6,5},{7,6},{8,11},{9,8},{10,9... | collective-permute-start | bytes 688136 | tf_op jit(solution)/shard_map/ppermute | solution.py:18
  34.3 12.7 %collective-permute-start.2 = (f16[128,896]{0,1:T(8,128)(2,1)S(1)}, f16[128,896]{0,1:T(8,128)(2,1)S(1)}, u32[]{:S(2)}, u32[]{:S(2)}) collective-permute-start(f16[128,896]{0,1:T(8,128)(2,1)S(1)} %fusion.62), channel_id=1, source_target_pairs={{0,1},{1,2},{2,3},{3,0},{4,5},{5,6},{6,7},{7,4},{8,9},{9,10},{10,1... | collective-permute-start | bytes 688136 | tf_op jit(solution)/shard_map/ppermute | solution.py:18
  34.5 19.6 %collective-permute-start.5 = (f16[128,896]{0,1:T(8,128)(2,1)S(1)}, f16[128,896]{0,1:T(8,128)(2,1)S(1)}, u32[]{:S(2)}, u32[]{:S(2)}) collective-permute-start(f16[128,896]{0,1:T(8,128)(2,1)S(1)} %fusion.59), channel_id=1, source_target_pairs={{0,3},{1,0},{2,1},{3,2},{4,7},{5,4},{6,5},{7,6},{8,11},{9,8},{10,9... | collective-permute-start | bytes 688136 | tf_op jit(solution)/shard_map/ppermute | solution.py:18
  38.0 42.1 %collective-permute-start.24 = (bf16[4,2,32,1024]{3,2,1,0:T(8,128)(2,1)S(1)}, bf16[4,2,32,1024]{3,2,1,0:T(8,128)(2,1)S(1)}, u32[]{:S(2)}, u32[]{:S(2)}) collective-permute-start(bf16[4,2,32,1024]{3,2,1,0:T(8,128)(2,1)S(1)} %pad_maximum_fusion.3), channel_id=1, source_target_pairs={{0,8},{4,12},{8,16},{12,20},{16,24},{20,28},{24,0},{28,4},{32,40},... | collective-permute-start | bytes 1572872 | tf_op jit(solution)/shard_map/ppermute | solution.py:42
  54.5 18.8 %collective-permute-start.6 = (f16[448,256]{1,0:T(8,128)(2,1)S(1)}, f16[448,256]{1,0:T(8,128)(2,1)S(1)}, u32[]{:S(2)}, u32[]{:S(2)}) collective-permute-start(f16[448,256]{1,0:T(8,128)(2,1)S(1)} %get-tuple-element.68), channel_id=1, source_target_pairs={{0,3},{1,0},{2,1},{3,2},{4,7},{5,4},{6,5},{7,6},{8,11},{9,8},{10,9... | collective-permute-start | bytes 688136 | tf_op jit(solution)/shard_map/ppermute | solution.py:18
  57.8 17.4 %collective-permute-start.8 = (f16[448,256]{1,0:T(8,128)(2,1)S(1)}, f16[448,256]{1,0:T(8,128)(2,1)S(1)}, u32[]{:S(2)}, u32[]{:S(2)}) collective-permute-start(f16[448,256]{1,0:T(8,128)(2,1)S(1)} %get-tuple-element.68), channel_id=1, source_target_pairs={{0,1},{1,2},{2,3},{3,0},{4,5},{5,6},{6,7},{7,4},{8,9},{9,10},{10,1... | collective-permute-start | bytes 688136 | tf_op jit(solution)/shard_map/ppermute | solution.py:18
  57.8 20.4 %collective-permute-start.7 = (f16[448,256]{1,0:T(8,128)(2,1)S(1)}, f16[448,256]{1,0:T(8,128)(2,1)S(1)}, u32[]{:S(2)}, u32[]{:S(2)}) collective-permute-start(f16[448,256]{1,0:T(8,128)(2,1)S(1)} %get-tuple-element.69), channel_id=1, source_target_pairs={{0,3},{1,0},{2,1},{3,2},{4,7},{5,4},{6,5},{7,6},{8,11},{9,8},{10,9... | collective-permute-start | bytes 688136 | tf_op jit(solution)/shard_map/ppermute | solution.py:18
  61.3 18.8 %collective-permute-start.11 = (f16[448,256]{1,0:T(8,128)(2,1)S(1)}, f16[448,256]{1,0:T(8,128)(2,1)S(1)}, u32[]{:S(2)}, u32[]{:S(2)}) collective-permute-start(f16[448,256]{1,0:T(8,128)(2,1)S(1)} %get-tuple-element.69), channel_id=1, source_target_pairs={{0,1},{1,2},{2,3},{3,0},{4,5},{5,6},{6,7},{7,4},{8,9},{9,10},{10,1... | collective-permute-start | bytes 688136 | tf_op jit(solution)/shard_map/ppermute | solution.py:18
  73.3 14.3 %collective-permute-start.23 = (bf16[4,2,32,1024]{3,2,1,0:T(8,128)(2,1)S(1)}, bf16[4,2,32,1024]{3,2,1,0:T(8,128)(2,1)S(1)}, u32[]{:S(2)}, u32[]{:S(2)}) collective-permute-start(bf16[4,2,32,1024]{3,2,1,0:T(8,128)(2,1)S(1)} %pad_maximum_fusion.3), channel_id=1, source_target_pairs={{0,16},{4,20},{8,24},{12,28},{16,0},{20,4},{24,8},{28,12},{32,48},... | collective-permute-start | bytes 1572872 | tf_op jit(solution)/shard_map/ppermute | solution.py:42
  75.2 22.5 %collective-permute-start.22 = (bf16[4,2,32,1024]{3,2,1,0:T(8,128)(2,1)S(1)}, bf16[4,2,32,1024]{3,2,1,0:T(8,128)(2,1)S(1)}, u32[]{:S(2)}, u32[]{:S(2)}) collective-permute-start(bf16[4,2,32,1024]{3,2,1,0:T(8,128)(2,1)S(1)} %pad_maximum_fusion.3), channel_id=1, source_target_pairs={{0,24},{4,28},{8,0},{12,4},{16,8},{20,12},{24,16},{28,20},{32,56},... | collective-permute-start | bytes 1572872 | tf_op jit(solution)/shard_map/ppermute | solution.py:42
  78.2 25.4 %collective-permute-start.21 = (bf16[4,2,32,1024]{3,2,1,0:T(8,128)(2,1)S(1)}, bf16[4,2,32,1024]{3,2,1,0:T(8,128)(2,1)S(1)}, u32[]{:S(2)}, u32[]{:S(2)}) collective-permute-start(bf16[4,2,32,1024]{3,2,1,0:T(8,128)(2,1)S(1)} %pad_maximum_fusion.2), channel_id=1, source_target_pairs={{0,64},{4,68},{8,72},{12,76},{16,80},{20,84},{24,88},{28,92},{32,9... | collective-permute-start | bytes 1572872 | tf_op jit(solution)/shard_map/ppermute | solution.py:42
  80.1 23.5 %collective-permute-start.20 = (bf16[4,2,32,1024]{3,2,1,0:T(8,128)(2,1)S(1)}, bf16[4,2,32,1024]{3,2,1,0:T(8,128)(2,1)S(1)}, u32[]{:S(2)}, u32[]{:S(2)}) collective-permute-start(bf16[4,2,32,1024]{3,2,1,0:T(8,128)(2,1)S(1)} %pad_maximum_fusion.2), channel_id=1, source_target_pairs={{0,128},{4,132},{8,136},{12,140},{16,144},{20,148},{24,152},{28,15... | collective-permute-start | bytes 1572872 | tf_op jit(solution)/shard_map/ppermute | solution.py:42
  80.1 23.9 %collective-permute-start.19 = (bf16[4,2,32,1024]{3,2,1,0:T(8,128)(2,1)S(1)}, bf16[4,2,32,1024]{3,2,1,0:T(8,128)(2,1)S(1)}, u32[]{:S(2)}, u32[]{:S(2)}) collective-permute-start(bf16[4,2,32,1024]{3,2,1,0:T(8,128)(2,1)S(1)} %pad_maximum_fusion.2), channel_id=1, source_target_pairs={{0,192},{4,196},{8,200},{12,204},{16,208},{20,212},{24,216},{28,22... | collective-permute-start | bytes 1572872 | tf_op jit(solution)/shard_map/ppermute | solution.py:42
  87.6 21.7 %collective-permute-start.9 = (f16[448,256]{1,0:T(8,128)(2,1)S(1)}, f16[448,256]{1,0:T(8,128)(2,1)S(1)}, u32[]{:S(2)}, u32[]{:S(2)}) collective-permute-start(f16[448,256]{1,0:T(8,128)(2,1)S(1)} %collective-permute-done.8), channel_id=1, source_target_pairs={{0,1},{1,2},{2,3},{3,0},{4,5},{5,6},{6,7},{7,4},{8,9},{9,10},{10,1... | collective-permute-start | bytes 688136 | tf_op jit(solution)/shard_map/ppermute | solution.py:18
  97.7 11.7 %collective-permute-start.10 = (f16[448,256]{1,0:T(8,128)(2,1)S(1)}, f16[448,256]{1,0:T(8,128)(2,1)S(1)}, u32[]{:S(2)}, u32[]{:S(2)}) collective-permute-start(f16[448,256]{1,0:T(8,128)(2,1)S(1)} %collective-permute-done.7), channel_id=1, source_target_pairs={{0,3},{1,0},{2,1},{3,2},{4,7},{5,4},{6,5},{7,6},{8,11},{9,8},{10,9... | collective-permute-start | bytes 688136 | tf_op jit(solution)/shard_map/ppermute | solution.py:18
  105.7 25.5 %collective-permute-start.26 = (bf16[4,4,2,32,1024]{4,3,2,1,0:T(8,128)(2,1)}, bf16[4,4,2,32,1024]{4,3,2,1,0:T(8,128)(2,1)S(1)}, u32[]{:S(2)}, u32[]{:S(2)}) collective-permute-start(bf16[4,4,2,32,1024]{4,3,2,1,0:T(8,128)(2,1)} %pad_maximum_fusion.1), channel_id=1, source_target_pairs={{0,4},{4,0},{8,12},{12,8},{16,20},{20,16},{24,28},{28,24},{32,36},... | collective-permute-start | bytes 6291464 | tf_op jit(solution)/shard_map/ppermute | solution.py:42
  109.3 22.8 %collective-permute-start.25 = (bf16[4,4,2,32,1024]{4,3,2,1,0:T(8,128)(2,1)}, bf16[4,4,2,32,1024]{4,3,2,1,0:T(8,128)(2,1)}, u32[]{:S(2)}, u32[]{:S(2)}) collective-permute-start(bf16[4,4,2,32,1024]{4,3,2,1,0:T(8,128)(2,1)} %get-tuple-element.63), channel_id=1, source_target_pairs={{0,4},{4,0},{8,12},{12,8},{16,20},{20,16},{24,28},{28,24},{32,36},... | collective-permute-start | bytes 6291464 | tf_op jit(solution)/shard_map/ppermute | solution.py:42
  111.7 34.5 %all-to-all-start = ((bf16[64,56,256]{2,1,0:T(8,128)(2,1)}), bf16[64,56,256]{2,1,0:T(8,128)(2,1)}, u32[]{:S(2)}, u32[]{:S(2)}) async-start(bf16[64,56,256]{2,1,0:T(8,128)(2,1)} %bitcast.5), calls=%async_computation | async-start | bytes 3670016 | tf_op jit(solution)/shard_map/all_to_all | solution.py:274
  (14 other events, 112.5 us)

commit v2 on v1

--- a/solution.py
+++ b/solution.py
@@ -157,11 +157,13 @@
     for i in range(group):
         codes = codes_ref[entries_ref[pl.program_id(0) * group + i]].astype(jnp.float32)
         assign.append(codes[0:1, :docs] * 64.0 + codes[0:1, docs:])
-    assign = jnp.concatenate(assign, axis=1).astype(jnp.int32) - first_ref[0]
-    low = assign & (LANES - 1)
-    high = assign - low
-    ids = lax.broadcasted_iota(jnp.int32, (LANES, docs * group), 0)
-    hot = jnp.where(low == ids, 1.0, 0.0).astype(jnp.bfloat16)
+    low = jnp.concatenate(assign, axis=0).astype(jnp.int32) & (LANES - 1)
+    down = low.T
+    ids = lax.broadcasted_iota(jnp.int32, (docs, LANES), 1)
+    hot = [jnp.where(down[:, i : i + 1] == ids, 1.0, 0.0).astype(jnp.bfloat16) for i in range(group)]
+    hot = jnp.concatenate(hot, axis=0)
+    high = jnp.concatenate(assign, axis=1).astype(jnp.int32) - first_ref[0]
+    high = high - (high & (LANES - 1))
     cols = jnp.concatenate([cols_ref[i] for i in range(group)], axis=1)
     ones = jnp.ones((8, docs * group), jnp.bfloat16)
     cols = jnp.concatenate([cols, ones], axis=0)
@@ -170,7 +172,7 @@
         mask = jnp.where(high == b * LANES, 1.0, 0.0).astype(jnp.bfloat16)
         picked.append(cols * mask)
     picked = jnp.concatenate(picked, axis=0)
-    got = lax.dot_general(picked, hot, (((1,), (1,)), ((), ())), preferred_element_type=jnp.float32)
+    got = jnp.dot(picked, hot, preferred_element_type=jnp.float32)
     for b in range(blocks):
         total[:, b * LANES : (b + 1) * LANES] += got[b * tall : (b + 1) * tall]
 
@@ -241,19 +243,20 @@
     centers = jnp.concatenate([centers, extra])
     ahead, behind = partial(1), partial(-1)
     low_a, top_b = ahead[half_docs:].astype(f16), behind[:half_docs].astype(f16)
-    lines = first_lines(centers, (low_a, top_b))
     near = (low_a, top_b)
     low_a, top_b = mp_shift(low_a, 1), mp_shift(top_b, -1)
     mine = partial(0)
     up, down = after((up, down), near, mine)
     top_a = (ahead[:half_docs] + up.astype(jnp.float32)).astype(f16)
     low_b = (behind[half_docs:] + down.astype(jnp.float32)).astype(f16)
-    lines = second_lines(*lines, (top_a, low_b))
+    hold = (top_a, low_b)
     top_a, low_b = mp_shift(top_a, 1), mp_shift(low_b, -1)
+    lines = first_lines(centers, hold)
     top = mine[:half_docs] + top_a.astype(jnp.float32) + top_b.astype(jnp.float32)
     low = mine[half_docs:] + low_a.astype(jnp.float32) + low_b.astype(jnp.float32)
     share = jnp.concatenate([top, low]).T.astype(f16)
     first_half, second_half = share[:half], share[half:]
+    lines = second_lines(*lines, (first_half, second_half))
     a_first = mp_shift(first_half, 1)
     b_second = mp_shift(second_half, -1)
     a_second = mp_shift(second_half, 1)
@@ -261,7 +264,6 @@
     c_first = mp_shift(a_first, 1)
     c_second = mp_shift(b_second, -1)
 
-    tables = gather_tables(*lines, (a_first, b_second, a_second, b_first))
     blocks, entries = table_order(index)
     parts = [first_half, second_half, b_first, b_second, c_first, c_second, a_first, a_second]
     i = jnp.arange(len(parts), dtype=jnp.int32)
@@ -275,6 +277,7 @@
         embedded.reshape(shards, feature_cols, docs), "dp", split_axis=0, concat_axis=0, tiled=True
     )
     ordered, doc_norms = put_in_order(blocks, embedded)
+    tables = gather_tables(*lines, doc_norms)
     upper = (feature_cols + 8) // 2
     tables = [t.reshape(shards // 2, upper, width) for t in tables]
     real = feature_cols - upper

time: 155 us -> 158 us (1.019)
  waiting for transfers between devices: 55.5 us -> 40.1 us
  starting transfers between devices: 51.3 us -> 63.5 us
  other arithmetic: 14.1 us -> 17.1 us
  Pallas kernels: 13.8 us -> 15.7 us
    ppermute x12, waiting for transfers between devices: 31.4 us -> 13.3 us  [mp_shift(): return lax.ppermute(value, 'mp', [(i, (i + step) % MP) for i in range(MP)])]
    ppermute x12, starting transfers between devices: 22.7 us -> 33.5 us  [mp_shift(): return lax.ppermute(value, 'mp', [(i, (i + step) % MP) for i in range(MP)])]
    all_to_all x1, waiting for transfers between devices: 6.7 us -> 11.1 us  [step(): lax.all_to_all(embedded.reshape(shards, feature_cols, docs), 'dp', split_...]
    pallas_call x1, Pallas kernels: 8.16 us -> 10 us  [new_state(): pl.pallas_call(sums_kernel, grid_spec=pltpu.PrefetchScalarGridSpec(num_sc...]
    ppermute x15, starting transfers between devices: 20.2 us -> 22 us  [dp_shift(): return lax.ppermute(value, 'dp', pairs)]
    ppermute x15, waiting for transfers between devices: 17.4 us -> 15.7 us  [dp_shift(): return lax.ppermute(value, 'dp', pairs)]
  transfers between devices with their start and end apart: 28 -> 28, of which waited for: 13 -> 8; matrix products, arithmetic and copies ran while one was open for 20% -> 21% of each run, Pallas kernels for 4% -> 4%
where the time goes in v2:
time: 158 us; the launch traced here: 157 us
  starting transfers between devices  63.5 us (40%)
  waiting for transfers between devices  40.1 us (25%)
  matrix products  17.3 us (11%)
  other arithmetic  17.1 us (11%)
  Pallas kernels  15.7 us (10%)
  local copies, waits for them, and re-layouts  2.08 us (1%)
    ppermute x12, starting transfers between devices, mp_shift(): return lax.ppermute(value, 'mp', [(i, (i + step) % MP) for i in range(MP)])  33.5 us
    ppermute x15, starting transfers between devices, dp_shift(): return lax.ppermute(value, 'dp', pairs)  22 us
    ppermute x15, waiting for transfers between devices, dp_shift(): return lax.ppermute(value, 'dp', pairs)  15.7 us
    ppermute x12, waiting for transfers between devices, mp_shift(): return lax.ppermute(value, 'mp', [(i, (i + step) % MP) for i in range(MP)])  13.3 us
    all_to_all x1, waiting for transfers between devices, step(): lax.all_to_all(embedded.reshape(shards, feature_cols, docs), 'dp', split_...  11.1 us
    pallas_call x1, Pallas kernels, new_state(): pl.pallas_call(sums_kernel, grid_spec=pltpu.PrefetchScalarGridSpec(num_sc...  10 us
    dot_general x4, matrix products, step(): lax.dot_general(part, rows, (((0,), (0,)), ((), ())), preferred_element_t...  8.91 us
    dot_general x4, matrix products, partial(): return jnp.dot(pooled, w, preferred_element_type=jnp.float32) * SCALE  8.42 us
  transfers between devices with their start and end apart: 28, of which 8 were waited for; matrix products, arithmetic and copies ran while one was open for 21% of the time, Pallas kernels for 4%

profile of v2, /device:TPU:1, one launch (start us, length us, event | category | flops | bytes accessed | tf_op | source)
XLA Modules:
  0.0 156.9 jit_solution(17385367311844467939)
XLA Ops:
  2.4 2.5 %collective-permute-start.12 = (bf16[64,1024]{1,0:T(8,128)(2,1)S(1)}, bf16[64,1024]{1,0:T(8,128)(2,1)}, u32[]{:S(2)}, u32[]{:S(2)}) collective-permute-start(bf16[64,1024]{1,0:T(8,128)(2,1)S(1)} %get-tuple-element.74), channel_id=1, source_target_pairs={{0,32},{4,36},{8,40},{12,44},{16,48},{20,52},{24,56},{28,60},{32,0... | collective-permute-start | bytes 393224 | tf_op jit(solution)/shard_map/ppermute | solution.py:42
  7.9 5.1 %collective-permute-start.1 = (f16[128,896]{0,1:T(8,128)(2,1)}, f16[128,896]{0,1:T(8,128)(2,1)S(1)}, u32[]{:S(2)}, u32[]{:S(2)}) collective-permute-start(f16[128,896]{0,1:T(8,128)(2,1)} %get-tuple-element.70), channel_id=1, source_target_pairs={{0,3},{1,0},{2,1},{3,2},{4,7},{5,4},{6,5},{7,6},{8,11},{9,8},{10,9... | collective-permute-start | bytes 688136 | tf_op jit(solution)/shard_map/ppermute | solution.py:18
  20.1 2.1 %collective-permute-start.3 = (f16[128,896]{0,1:T(8,128)(2,1)}, f16[128,896]{0,1:T(8,128)(2,1)S(1)}, u32[]{:S(2)}, u32[]{:S(2)}) collective-permute-start(f16[128,896]{0,1:T(8,128)(2,1)} %slice_convert_fusion), channel_id=1, source_target_pairs={{0,3},{1,0},{2,1},{3,2},{4,7},{5,4},{6,5},{7,6},{8,11},{9,8},{10,9... | collective-permute-start | bytes 688136 | tf_op jit(solution)/shard_map/ppermute | solution.py:18
  22.3 2.1 %fusion.13 = f32[256,896]{0,1:T(8,128)S(1)} fusion(bf16[256,896]{1,0:T(8,128)(2,1)S(1)} %copy-done, bf16[896,3584]{1,0:T(8,128)(2,1)} %param.6, s32[]{:T(128)S(6)} %select_n.165), kind=kOutput, calls=%fused_computation.19 | convolution fusion | flops 411271168 | bytes 2981892 | tf_op jit(solution)/shard_map/dot_general | solution.py:234
  26.6 3.2 %collective-permute-start.5 = (f16[128,896]{0,1:T(8,128)(2,1)S(1)}, f16[128,896]{0,1:T(8,128)(2,1)S(1)}, u32[]{:S(2)}, u32[]{:S(2)}) collective-permute-start(f16[128,896]{0,1:T(8,128)(2,1)S(1)} %fusion.59), channel_id=1, source_target_pairs={{0,3},{1,0},{2,1},{3,2},{4,7},{5,4},{6,5},{7,6},{8,11},{9,8},{10,9... | collective-permute-start | bytes 688136 | tf_op jit(solution)/shard_map/ppermute | solution.py:18
  32.6 2.5 %collective-permute-start.17 = (bf16[2,32,1024]{2,1,0:T(8,128)(2,1)S(1)}, bf16[2,32,1024]{2,1,0:T(8,128)(2,1)S(1)}, u32[]{:S(2)}, u32[]{:S(2)}) collective-permute-start(bf16[2,32,1024]{2,1,0:T(8,128)(2,1)S(1)} %get-tuple-element.39), channel_id=1, source_target_pairs={{0,128},{4,132},{8,136},{12,140},{16,144},{20,148},{24,152},{28,15... | collective-permute-start | bytes 393224 | tf_op jit(solution)/shard_map/ppermute | solution.py:42
  36.2 3.5 %collective-permute-done.2 = f16[128,896]{0,1:T(8,128)(2,1)S(1)} collective-permute-done((f16[128,896]{0,1:T(8,128)(2,1)S(1)}, f16[128,896]{0,1:T(8,128)(2,1)S(1)}, u32[]{:S(2)}, u32[]{:S(2)}) %collective-permute-start.2) | collective-permute-done | bytes 229408 | tf_op jit(solution)/shard_map/ppermute | solution.py:18
  41.0 2.6 %collective-permute-start.14 = (bf16[2,32,1024]{2,1,0:T(8,128)(2,1)S(1)}, bf16[2,32,1024]{2,1,0:T(8,128)(2,1)S(1)}, u32[]{:S(2)}, u32[]{:S(2)}) collective-permute-start(bf16[2,32,1024]{2,1,0:T(8,128)(2,1)S(1)} %get-tuple-element.35), channel_id=1, source_target_pairs={{0,16},{4,20},{8,24},{12,28},{16,0},{20,4},{24,8},{28,12},{32,48},... | collective-permute-start | bytes 393224 | tf_op jit(solution)/shard_map/ppermute | solution.py:42
  45.5 2.9 %collective-permute-start.8 = (f16[448,256]{1,0:T(8,128)(2,1)S(1)}, f16[448,256]{1,0:T(8,128)(2,1)S(1)}, u32[]{:S(2)}, u32[]{:S(2)}) collective-permute-start(f16[448,256]{1,0:T(8,128)(2,1)S(1)} %get-tuple-element.68), channel_id=1, source_target_pairs={{0,1},{1,2},{2,3},{3,0},{4,5},{5,6},{6,7},{7,4},{8,9},{9,10},{10,1... | collective-permute-start | bytes 688136 | tf_op jit(solution)/shard_map/ppermute | solution.py:18
  57.6 13.8 %collective-permute-start.9 = (f16[448,256]{1,0:T(8,128)(2,1)S(1)}, f16[448,256]{1,0:T(8,128)(2,1)S(1)}, u32[]{:S(2)}, u32[]{:S(2)}) collective-permute-start(f16[448,256]{1,0:T(8,128)(2,1)S(1)} %collective-permute-done.8), channel_id=1, source_target_pairs={{0,1},{1,2},{2,3},{3,0},{4,5},{5,6},{6,7},{7,4},{8,9},{9,10},{10,1... | collective-permute-start | bytes 688136 | tf_op jit(solution)/shard_map/ppermute | solution.py:18
  71.7 2.8 %collective-permute-done.9 = f16[448,256]{1,0:T(8,128)(2,1)S(1)} collective-permute-done((f16[448,256]{1,0:T(8,128)(2,1)S(1)}, f16[448,256]{1,0:T(8,128)(2,1)S(1)}, u32[]{:S(2)}, u32[]{:S(2)}) %collective-permute-start.9) | collective-permute-done | bytes 229408 | tf_op jit(solution)/shard_map/ppermute | solution.py:18
  75.3 5.0 %collective-permute-done.10 = f16[448,256]{1,0:T(8,128)(2,1)S(1)} collective-permute-done((f16[448,256]{1,0:T(8,128)(2,1)S(1)}, f16[448,256]{1,0:T(8,128)(2,1)S(1)}, u32[]{:S(2)}, u32[]{:S(2)}) %collective-permute-start.10) | collective-permute-done | bytes 229408 | tf_op jit(solution)/shard_map/ppermute | solution.py:18
  80.3 2.8 %collective-permute-start.20 = (bf16[4,2,32,1024]{3,2,1,0:T(8,128)(2,1)S(1)}, bf16[4,2,32,1024]{3,2,1,0:T(8,128)(2,1)}, u32[]{:S(2)}, u32[]{:S(2)}) collective-permute-start(bf16[4,2,32,1024]{3,2,1,0:T(8,128)(2,1)S(1)} %pad_maximum_fusion.2), channel_id=1, source_target_pairs={{0,128},{4,132},{8,136},{12,140},{16,144},{20,148},{24,152},{28,15... | collective-permute-start | bytes 1572872 | tf_op jit(solution)/shard_map/ppermute | solution.py:42
  85.7 3.8 %put_in_order.1 = (bf16[4096,256]{1,0:T(8,128)(2,1)}, f32[1,256]{1,0:T(1,128)}) custom-call(s32[128]{0:T(128)} %pad_add_fusion.blocks_ref, bf16[3584,256]{1,0:T(8,128)(2,1)} %put_in_place.1.whole_ref), custom_call_target="tpu_custom_call" | custom-call | flops 3000000 | bytes 3670016 | tf_op jit(solution)/shard_map/put_in_order/pallas_call | solution.py:135
  89.5 2.4 %collective-permute-done.20 = bf16[4,2,32,1024]{3,2,1,0:T(8,128)(2,1)} collective-permute-done((bf16[4,2,32,1024]{3,2,1,0:T(8,128)(2,1)S(1)}, bf16[4,2,32,1024]{3,2,1,0:T(8,128)(2,1)}, u32[]{:S(2)}, u32[]{:S(2)}) %collective-permute-start.20) | collective-permute-done | bytes 524320 | tf_op jit(solution)/shard_map/ppermute | solution.py:42
  91.9 13.2 %collective-permute-done.19 = bf16[4,2,32,1024]{3,2,1,0:T(8,128)(2,1)} collective-permute-done((bf16[4,2,32,1024]{3,2,1,0:T(8,128)(2,1)S(1)}, bf16[4,2,32,1024]{3,2,1,0:T(8,128)(2,1)}, u32[]{:S(2)}, u32[]{:S(2)}) %collective-permute-start.19) | collective-permute-done | bytes 524320 | tf_op jit(solution)/shard_map/ppermute | solution.py:42
  106.8 2.5 %collective-permute-start.26 = (bf16[4,4,2,32,1024]{4,3,2,1,0:T(8,128)(2,1)}, bf16[4,4,2,32,1024]{4,3,2,1,0:T(8,128)(2,1)S(1)}, u32[]{:S(2)}, u32[]{:S(2)}) collective-permute-start(bf16[4,4,2,32,1024]{4,3,2,1,0:T(8,128)(2,1)} %pad_maximum_fusion.1), channel_id=1, source_target_pairs={{0,4},{4,0},{8,12},{12,8},{16,20},{20,16},{24,28},{28,24},{32,36},... | collective-permute-start | bytes 6291464 | tf_op jit(solution)/shard_map/ppermute | solution.py:42
  109.3 3.4 %multiply_reduce_fusion.3 = (f32[1024]{0:T(1024)S(1)}, bf16[4,4,2,32,1024]{4,3,2,1,0:T(8,128)(2,1)}) fusion(bf16[1,4,2,32,1024]{4,3,2,1,0:T(8,128)(2,1)} %bitcast.21, bf16[1,4,2,32,1024]{4,3,2,1,0:T(8,128)(2,1)} %bitcast.20, bf16[1,4,2,32,1024]{4,3,2,1,0:T(8,128)(2,1)} %bitcast.19, bf16[1,4,2,32,1024]{4,3,2,1,0:T(8,128)(2,1)S(1)} %bitcast.60), kind=kLoop, calls=%fused_computation.3 | loop fusion | flops 6290432 | bytes 4198400 | tf_op jit(solution)/shard_map/reduce_sum | solution.py:290
  112.7 8.0 %all-to-all-start = ((bf16[64,56,256]{2,1,0:T(8,128)(2,1)}), bf16[64,56,256]{2,1,0:T(8,128)(2,1)}, u32[]{:S(2)}, u32[]{:S(2)}) async-start(bf16[64,56,256]{2,1,0:T(8,128)(2,1)} %bitcast.5), calls=%async_computation | async-start | bytes 3670016 | tf_op jit(solution)/shard_map/all_to_all | solution.py:276
  122.5 2.5 %fusion.41 = f32[256,1024]{1,0:T(8,128)S(1)} fusion(bf16[1024,1024]{1,0:T(8,128)(2,1)} %bitcast.26, bf16[4096,256]{1,0:T(8,128)(2,1)} %get-tuple-element.51), kind=kOutput, calls=%fused_computation.51 | convolution fusion | flops 536870912 | bytes 3670016 | tf_op jit(solution)/shard_map/dot_general | solution.py:293
  125.0 2.3 %convolution_add_fusion.1 = f32[256,1024]{1,0:T(8,128)S(1)} fusion(f32[256,1024]{1,0:T(8,128)S(1)} %fusion.41, bf16[1024,1024]{1,0:T(8,128)(2,1)} %bitcast.27, bf16[4096,256]{1,0:T(8,128)(2,1)S(1)} %copy-done.1), kind=kOutput, calls=%fused_computation.17 | convolution fusion | flops 537133056 | bytes 4718592 | tf_op jit(solution)/shard_map/dot_general | solution.py:293
  132.4 3.4 %add_subtract_fusion = f32[256,1024]{1,0:T(8,128)} fusion(f32[256,1024]{1,0:T(8,128)S(1)} %fusion.37, f32[256,1024]{1,0:T(8,128)S(1)} %convolution_add_fusion.1, bf16[1024,1024]{1,0:T(8,128)(2,1)} %bitcast.28, bf16[4096,256]{1,0:T(8,128)(2,1)S(1)} %copy-done.1, f32[1024]{0:T(1024)S(1)} %add_add_fusion, f32[256]{0:T(256)S(1)} %bitcast.76), kind=kOutput, calls=%fused_computation.27 | convolution fusion | flops 538181632 | bytes 5772288 | tf_op jit(solution)/shard_map/dot_general | solution.py:293
  135.7 11.1 %all-to-all-done.cols_ref = bf16[64,56,256]{2,1,0:T(8,128)(2,1)} async-done(((bf16[64,56,256]{2,1,0:T(8,128)(2,1)}), bf16[64,56,256]{2,1,0:T(8,128)(2,1)}, u32[]{:S(2)}, u32[]{:S(2)}) %all-to-all-start) | async-done | bytes 1835040 | tf_op jit(solution)/shard_map/all_to_all | solution.py:276
  146.9 10.0 %new_state.1 = (f32[56,1024]{1,0:T(8,128)}, f32[1,1024]{1,0:T(1,128)}, bf16[56,1024]{1,0:T(8,128)(2,1)}) custom-call(s32[1]{0:T(128)} %bitcast.32.first_ref, s32[64]{0:T(128)} %fusion.80.entries_ref, bf16[64,8,512]{2,1,0:T(8,128)(2,1)} %pad_maximum_fusion.4.codes_ref, bf16[64,56,256]{2,1,0:T(8,128)(2,1)} %all-to-all-done.cols_ref, f32[56,1024]{1,0:T(8,128)} %bitcast.69, ...), custom_call_target="tpu_custom_call" | custom-call | flops 1879048192 | bytes 1835008 | tf_op jit(solution)/shard_map/new_state/pallas_call | solution.py:196
  (105 shorter events, 42.1 us)
Async XLA Ops:
  2.4 27.9 %collective-permute-start.12 = (bf16[64,1024]{1,0:T(8,128)(2,1)S(1)}, bf16[64,1024]{1,0:T(8,128)(2,1)}, u32[]{:S(2)}, u32[]{:S(2)}) collective-permute-start(bf16[64,1024]{1,0:T(8,128)(2,1)S(1)} %get-tuple-element.74), channel_id=1, source_target_pairs={{0,32},{4,36},{8,40},{12,44},{16,48},{20,52},{24,56},{28,60},{32,0... | collective-permute-start | bytes 393224 | tf_op jit(solution)/shard_map/ppermute | solution.py:42
  7.9 16.6 %collective-permute-start.1 = (f16[128,896]{0,1:T(8,128)(2,1)}, f16[128,896]{0,1:T(8,128)(2,1)S(1)}, u32[]{:S(2)}, u32[]{:S(2)}) collective-permute-start(f16[128,896]{0,1:T(8,128)(2,1)} %get-tuple-element.70), channel_id=1, source_target_pairs={{0,3},{1,0},{2,1},{3,2},{4,7},{5,4},{6,5},{7,6},{8,11},{9,8},{10,9... | collective-permute-start | bytes 688136 | tf_op jit(solution)/shard_map/ppermute | solution.py:18
  13.0 12.1 %collective-permute-start = (f16[128,896]{0,1:T(8,128)(2,1)S(1)}, f16[128,896]{0,1:T(8,128)(2,1)}, u32[]{:S(2)}, u32[]{:S(2)}) collective-permute-start(f16[128,896]{0,1:T(8,128)(2,1)S(1)} %get-tuple-element.71), channel_id=1, source_target_pairs={{0,1},{1,2},{2,3},{3,0},{4,5},{5,6},{6,7},{7,4},{8,9},{9,10},{10,1... | collective-permute-start | bytes 688136 | tf_op jit(solution)/shard_map/ppermute | solution.py:18
  15.8 16.7 %collective-permute-start.4 = (f16[128,896]{0,1:T(8,128)(2,1)}, f16[128,896]{0,1:T(8,128)(2,1)S(1)}, u32[]{:S(2)}, u32[]{:S(2)}) collective-permute-start(f16[128,896]{0,1:T(8,128)(2,1)} %slice_convert_fusion.1), channel_id=1, source_target_pairs={{0,1},{1,2},{2,3},{3,0},{4,5},{5,6},{6,7},{7,4},{8,9},{9,10},{10,1... | collective-permute-start | bytes 688136 | tf_op jit(solution)/shard_map/ppermute | solution.py:18
  20.1 14.9 %collective-permute-start.3 = (f16[128,896]{0,1:T(8,128)(2,1)}, f16[128,896]{0,1:T(8,128)(2,1)S(1)}, u32[]{:S(2)}, u32[]{:S(2)}) collective-permute-start(f16[128,896]{0,1:T(8,128)(2,1)} %slice_convert_fusion), channel_id=1, source_target_pairs={{0,3},{1,0},{2,1},{3,2},{4,7},{5,4},{6,5},{7,6},{8,11},{9,8},{10,9... | collective-permute-start | bytes 688136 | tf_op jit(solution)/shard_map/ppermute | solution.py:18
  26.1 13.6 %collective-permute-start.2 = (f16[128,896]{0,1:T(8,128)(2,1)S(1)}, f16[128,896]{0,1:T(8,128)(2,1)S(1)}, u32[]{:S(2)}, u32[]{:S(2)}) collective-permute-start(f16[128,896]{0,1:T(8,128)(2,1)S(1)} %fusion.62), channel_id=1, source_target_pairs={{0,1},{1,2},{2,3},{3,0},{4,5},{5,6},{6,7},{7,4},{8,9},{9,10},{10,1... | collective-permute-start | bytes 688136 | tf_op jit(solution)/shard_map/ppermute | solution.py:18
  26.6 14.4 %collective-permute-start.5 = (f16[128,896]{0,1:T(8,128)(2,1)S(1)}, f16[128,896]{0,1:T(8,128)(2,1)S(1)}, u32[]{:S(2)}, u32[]{:S(2)}) collective-permute-start(f16[128,896]{0,1:T(8,128)(2,1)S(1)} %fusion.59), channel_id=1, source_target_pairs={{0,3},{1,0},{2,1},{3,2},{4,7},{5,4},{6,5},{7,6},{8,11},{9,8},{10,9... | collective-permute-start | bytes 688136 | tf_op jit(solution)/shard_map/ppermute | solution.py:18
  31.3 12.7 %collective-permute-start.18 = (bf16[2,32,1024]{2,1,0:T(8,128)(2,1)S(1)}, bf16[2,32,1024]{2,1,0:T(8,128)(2,1)S(1)}, u32[]{:S(2)}, u32[]{:S(2)}) collective-permute-start(bf16[2,32,1024]{2,1,0:T(8,128)(2,1)S(1)} %get-tuple-element.39), channel_id=1, source_target_pairs={{0,64},{4,68},{8,72},{12,76},{16,80},{20,84},{24,88},{28,92},{32,9... | collective-permute-start | bytes 393224 | tf_op jit(solution)/shard_map/ppermute | solution.py:42
  32.6 12.9 %collective-permute-start.17 = (bf16[2,32,1024]{2,1,0:T(8,128)(2,1)S(1)}, bf16[2,32,1024]{2,1,0:T(8,128)(2,1)S(1)}, u32[]{:S(2)}, u32[]{:S(2)}) collective-permute-start(bf16[2,32,1024]{2,1,0:T(8,128)(2,1)S(1)} %get-tuple-element.39), channel_id=1, source_target_pairs={{0,128},{4,132},{8,136},{12,140},{16,144},{20,148},{24,152},{28,15... | collective-permute-start | bytes 393224 | tf_op jit(solution)/shard_map/ppermute | solution.py:42
  35.0 13.4 %collective-permute-start.16 = (bf16[2,32,1024]{2,1,0:T(8,128)(2,1)S(1)}, bf16[2,32,1024]{2,1,0:T(8,128)(2,1)S(1)}, u32[]{:S(2)}, u32[]{:S(2)}) collective-permute-start(bf16[2,32,1024]{2,1,0:T(8,128)(2,1)S(1)} %get-tuple-element.39), channel_id=1, source_target_pairs={{0,192},{4,196},{8,200},{12,204},{16,208},{20,212},{24,216},{28,22... | collective-permute-start | bytes 393224 | tf_op jit(solution)/shard_map/ppermute | solution.py:42
  39.7 9.4 %collective-permute-start.15 = (bf16[2,32,1024]{2,1,0:T(8,128)(2,1)S(1)}, bf16[2,32,1024]{2,1,0:T(8,128)(2,1)S(1)}, u32[]{:S(2)}, u32[]{:S(2)}) collective-permute-start(bf16[2,32,1024]{2,1,0:T(8,128)(2,1)S(1)} %get-tuple-element.35), channel_id=1, source_target_pairs={{0,8},{4,12},{8,16},{12,20},{16,24},{20,28},{24,0},{28,4},{32,40},... | collective-permute-start | bytes 393224 | tf_op jit(solution)/shard_map/ppermute | solution.py:42
  41.0 9.7 %collective-permute-start.14 = (bf16[2,32,1024]{2,1,0:T(8,128)(2,1)S(1)}, bf16[2,32,1024]{2,1,0:T(8,128)(2,1)S(1)}, u32[]{:S(2)}, u32[]{:S(2)}) collective-permute-start(bf16[2,32,1024]{2,1,0:T(8,128)(2,1)S(1)} %get-tuple-element.35), channel_id=1, source_target_pairs={{0,16},{4,20},{8,24},{12,28},{16,0},{20,4},{24,8},{28,12},{32,48},... | collective-permute-start | bytes 393224 | tf_op jit(solution)/shard_map/ppermute | solution.py:42
  49.1 22.4 %collective-permute-start.11 = (f16[448,256]{1,0:T(8,128)(2,1)S(1)}, f16[448,256]{1,0:T(8,128)(2,1)S(1)}, u32[]{:S(2)}, u32[]{:S(2)}) collective-permute-start(f16[448,256]{1,0:T(8,128)(2,1)S(1)} %get-tuple-element.69), channel_id=1, source_target_pairs={{0,1},{1,2},{2,3},{3,0},{4,5},{5,6},{6,7},{7,4},{8,9},{9,10},{10,1... | collective-permute-start | bytes 688136 | tf_op jit(solution)/shard_map/ppermute | solution.py:18
  52.8 30.5 %collective-permute-start.24 = (bf16[4,2,32,1024]{3,2,1,0:T(8,128)(2,1)S(1)}, bf16[4,2,32,1024]{3,2,1,0:T(8,128)(2,1)S(1)}, u32[]{:S(2)}, u32[]{:S(2)}) collective-permute-start(bf16[4,2,32,1024]{3,2,1,0:T(8,128)(2,1)S(1)} %pad_maximum_fusion.3), channel_id=1, source_target_pairs={{0,8},{4,12},{8,16},{12,20},{16,24},{20,28},{24,0},{28,4},{32,40},... | collective-permute-start | bytes 1572872 | tf_op jit(solution)/shard_map/ppermute | solution.py:42
  53.5 36.0 %collective-permute-start.23 = (bf16[4,2,32,1024]{3,2,1,0:T(8,128)(2,1)S(1)}, bf16[4,2,32,1024]{3,2,1,0:T(8,128)(2,1)S(1)}, u32[]{:S(2)}, u32[]{:S(2)}) collective-permute-start(bf16[4,2,32,1024]{3,2,1,0:T(8,128)(2,1)S(1)} %pad_maximum_fusion.3), channel_id=1, source_target_pairs={{0,16},{4,20},{8,24},{12,28},{16,0},{20,4},{24,8},{28,12},{32,48},... | collective-permute-start | bytes 1572872 | tf_op jit(solution)/shard_map/ppermute | solution.py:42
  54.4 35.0 %collective-permute-start.22 = (bf16[4,2,32,1024]{3,2,1,0:T(8,128)(2,1)S(1)}, bf16[4,2,32,1024]{3,2,1,0:T(8,128)(2,1)S(1)}, u32[]{:S(2)}, u32[]{:S(2)}) collective-permute-start(bf16[4,2,32,1024]{3,2,1,0:T(8,128)(2,1)S(1)} %pad_maximum_fusion.3), channel_id=1, source_target_pairs={{0,24},{4,28},{8,0},{12,4},{16,8},{20,12},{24,16},{28,20},{32,56},... | collective-permute-start | bytes 1572872 | tf_op jit(solution)/shard_map/ppermute | solution.py:42
  57.6 16.8 %collective-permute-start.9 = (f16[448,256]{1,0:T(8,128)(2,1)S(1)}, f16[448,256]{1,0:T(8,128)(2,1)S(1)}, u32[]{:S(2)}, u32[]{:S(2)}) collective-permute-start(f16[448,256]{1,0:T(8,128)(2,1)S(1)} %collective-permute-done.8), channel_id=1, source_target_pairs={{0,1},{1,2},{2,3},{3,0},{4,5},{5,6},{6,7},{7,4},{8,9},{9,10},{10,1... | collective-permute-start | bytes 688136 | tf_op jit(solution)/shard_map/ppermute | solution.py:18
  71.5 8.8 %collective-permute-start.10 = (f16[448,256]{1,0:T(8,128)(2,1)S(1)}, f16[448,256]{1,0:T(8,128)(2,1)S(1)}, u32[]{:S(2)}, u32[]{:S(2)}) collective-permute-start(f16[448,256]{1,0:T(8,128)(2,1)S(1)} %collective-permute-done.7), channel_id=1, source_target_pairs={{0,3},{1,0},{2,1},{3,2},{4,7},{5,4},{6,5},{7,6},{8,11},{9,8},{10,9... | collective-permute-start | bytes 688136 | tf_op jit(solution)/shard_map/ppermute | solution.py:18
  74.4 15.0 %collective-permute-start.21 = (bf16[4,2,32,1024]{3,2,1,0:T(8,128)(2,1)S(1)}, bf16[4,2,32,1024]{3,2,1,0:T(8,128)(2,1)}, u32[]{:S(2)}, u32[]{:S(2)}) collective-permute-start(bf16[4,2,32,1024]{3,2,1,0:T(8,128)(2,1)S(1)} %pad_maximum_fusion.2), channel_id=1, source_target_pairs={{0,64},{4,68},{8,72},{12,76},{16,80},{20,84},{24,88},{28,92},{32,9... | collective-permute-start | bytes 1572872 | tf_op jit(solution)/shard_map/ppermute | solution.py:42
  80.3 11.6 %collective-permute-start.20 = (bf16[4,2,32,1024]{3,2,1,0:T(8,128)(2,1)S(1)}, bf16[4,2,32,1024]{3,2,1,0:T(8,128)(2,1)}, u32[]{:S(2)}, u32[]{:S(2)}) collective-permute-start(bf16[4,2,32,1024]{3,2,1,0:T(8,128)(2,1)S(1)} %pad_maximum_fusion.2), channel_id=1, source_target_pairs={{0,128},{4,132},{8,136},{12,140},{16,144},{20,148},{24,152},{28,15... | collective-permute-start | bytes 1572872 | tf_op jit(solution)/shard_map/ppermute | solution.py:42
  83.3 21.9 %collective-permute-start.19 = (bf16[4,2,32,1024]{3,2,1,0:T(8,128)(2,1)S(1)}, bf16[4,2,32,1024]{3,2,1,0:T(8,128)(2,1)}, u32[]{:S(2)}, u32[]{:S(2)}) collective-permute-start(bf16[4,2,32,1024]{3,2,1,0:T(8,128)(2,1)S(1)} %pad_maximum_fusion.2), channel_id=1, source_target_pairs={{0,192},{4,196},{8,200},{12,204},{16,208},{20,212},{24,216},{28,22... | collective-permute-start | bytes 1572872 | tf_op jit(solution)/shard_map/ppermute | solution.py:42
  106.8 20.6 %collective-permute-start.26 = (bf16[4,4,2,32,1024]{4,3,2,1,0:T(8,128)(2,1)}, bf16[4,4,2,32,1024]{4,3,2,1,0:T(8,128)(2,1)S(1)}, u32[]{:S(2)}, u32[]{:S(2)}) collective-permute-start(bf16[4,4,2,32,1024]{4,3,2,1,0:T(8,128)(2,1)} %pad_maximum_fusion.1), channel_id=1, source_target_pairs={{0,4},{4,0},{8,12},{12,8},{16,20},{20,16},{24,28},{28,24},{32,36},... | collective-permute-start | bytes 6291464 | tf_op jit(solution)/shard_map/ppermute | solution.py:42
  112.7 15.5 %collective-permute-start.25 = (bf16[4,4,2,32,1024]{4,3,2,1,0:T(8,128)(2,1)}, bf16[4,4,2,32,1024]{4,3,2,1,0:T(8,128)(2,1)}, u32[]{:S(2)}, u32[]{:S(2)}) collective-permute-start(bf16[4,4,2,32,1024]{4,3,2,1,0:T(8,128)(2,1)} %get-tuple-element.63), channel_id=1, source_target_pairs={{0,4},{4,0},{8,12},{12,8},{16,20},{20,16},{24,28},{28,24},{32,36},... | collective-permute-start | bytes 6291464 | tf_op jit(solution)/shard_map/ppermute | solution.py:42
  112.7 34.2 %all-to-all-start = ((bf16[64,56,256]{2,1,0:T(8,128)(2,1)}), bf16[64,56,256]{2,1,0:T(8,128)(2,1)}, u32[]{:S(2)}, u32[]{:S(2)}) async-start(bf16[64,56,256]{2,1,0:T(8,128)(2,1)} %bitcast.5), calls=%async_computation | async-start | bytes 3670016 | tf_op jit(solution)/shard_map/all_to_all | solution.py:276
  (15 other events, 135.0 us)

commit v3 on v1

--- a/solution.py
+++ b/solution.py
@@ -49,12 +49,13 @@
 def first_lines(piece, hold):
     half = piece.shape[0] // 2
     pair = jnp.stack([piece, after(dp_shift(piece, 1, 1), hold)])
-    return shifts(pair[:, :half], 2), shifts(pair[:, half:], 0)
-
-
-def second_lines(upper, lower, hold):
-    upper, lower = after((upper, lower), hold)
-    return shifts(jnp.stack(upper), 0), shifts(jnp.stack(lower), 2)
+    upper = shifts(pair[:, :half], 2)
+    lower = shifts(pair[:, half:], 0)
+    return upper, lower
+
+
+def second_lines(line, dim, hold):
+    return shifts(jnp.stack(after(line, hold)), dim)
 
 
 def gather_tables(upper, lower, hold):
@@ -156,7 +157,7 @@
     assign = []
     for i in range(group):
         codes = codes_ref[entries_ref[pl.program_id(0) * group + i]].astype(jnp.float32)
-        assign.append(codes[0:1, :docs] * 64.0 + codes[0:1, docs:])
+        assign.append(codes[0:1, :docs] * 64.0 + codes[0:1, docs : 2 * docs])
     assign = jnp.concatenate(assign, axis=1).astype(jnp.int32) - first_ref[0]
     low = assign & (LANES - 1)
     high = assign - low
@@ -186,7 +187,7 @@
 def new_state(first, entries, codes, cols, ema_sums, ema_counts):
     shards, rows, docs = cols.shape
     width = ema_counts.shape[1]
-    group = 8
+    group = 32
 
     def all_of(shape):
         return pl.BlockSpec(shape, lambda i, f, e: (0,) * len(shape))
@@ -237,23 +238,32 @@
     sums_t = ema_sums.T
     centers = (sums_t / ema_counts[None, :]).astype(jnp.bfloat16)
     pair = jnp.stack([assignments // 64, assignments % 64]).astype(jnp.bfloat16).reshape(1, 2 * docs)
-    extra = jnp.pad(pair, ((0, 7), (0, width - 2 * docs)))
-    centers = jnp.concatenate([centers, extra])
+    wide = centers.astype(jnp.float32)
+    norms = jnp.sum(wide * wide, axis=0, keepdims=True)
+    extra = [jnp.pad(pair, ((0, 0), (0, width - 2 * docs)))]
+    for _ in range(3):
+        coarse = lax.reduce_precision(norms, 8, 7)
+        extra.append(coarse.astype(jnp.bfloat16))
+        norms = norms - coarse
+    extra.append(jnp.zeros((4, width), jnp.bfloat16))
+    centers = jnp.concatenate([centers] + extra)
     ahead, behind = partial(1), partial(-1)
     low_a, top_b = ahead[half_docs:].astype(f16), behind[:half_docs].astype(f16)
-    lines = first_lines(centers, (low_a, top_b))
     near = (low_a, top_b)
     low_a, top_b = mp_shift(low_a, 1), mp_shift(top_b, -1)
     mine = partial(0)
     up, down = after((up, down), near, mine)
     top_a = (ahead[:half_docs] + up.astype(jnp.float32)).astype(f16)
     low_b = (behind[half_docs:] + down.astype(jnp.float32)).astype(f16)
-    lines = second_lines(*lines, (top_a, low_b))
+    hold = (top_a, low_b)
     top_a, low_b = mp_shift(top_a, 1), mp_shift(low_b, -1)
+    upper, lower = first_lines(centers, hold)
+    upper = second_lines(upper, 0, hold)
     top = mine[:half_docs] + top_a.astype(jnp.float32) + top_b.astype(jnp.float32)
     low = mine[half_docs:] + low_a.astype(jnp.float32) + low_b.astype(jnp.float32)
     share = jnp.concatenate([top, low]).T.astype(f16)
     first_half, second_half = share[:half], share[half:]
+    lower = second_lines(lower, 2, (first_half, second_half))
     a_first = mp_shift(first_half, 1)
     b_second = mp_shift(second_half, -1)
     a_second = mp_shift(second_half, 1)
@@ -261,7 +271,6 @@
     c_first = mp_shift(a_first, 1)
     c_second = mp_shift(b_second, -1)
 
-    tables = gather_tables(*lines, (a_first, b_second, a_second, b_first))
     blocks, entries = table_order(index)
     parts = [first_half, second_half, b_first, b_second, c_first, c_second, a_first, a_second]
     i = jnp.arange(len(parts), dtype=jnp.int32)
@@ -275,16 +284,14 @@
         embedded.reshape(shards, feature_cols, docs), "dp", split_axis=0, concat_axis=0, tiled=True
     )
     ordered, doc_norms = put_in_order(blocks, embedded)
+    tables = gather_tables(upper, lower, doc_norms)
     upper = (feature_cols + 8) // 2
     tables = [t.reshape(shards // 2, upper, width) for t in tables]
     real = feature_cols - upper
-    codes = jnp.concatenate([t[:, real:, : 2 * docs] for t in tables[1::2]])
-    center_norms, products = 0.0, 0.0
+    codes = jnp.concatenate([t[:, real:, :] for t in tables[1::2]])
+    center_norms = jnp.sum(codes[:, 1:4].astype(jnp.float32), axis=(0, 1))
+    products = 0.0
     for i, table in enumerate(tables):
-        wide = table.astype(jnp.float32)
-        if i % 2:
-            wide = jnp.where(lax.broadcasted_iota(jnp.int32, table.shape, 1) < real, wide, 0.0)
-        center_norms = center_norms + jnp.sum(wide * wide, axis=(0, 1))
         rows = table.reshape(-1, width)
         part = ordered[i * rows.shape[0] : (i + 1) * rows.shape[0]]
         products = products + lax.dot_general(part, rows, (((0,), (0,)), ((), ())), preferred_element_type=jnp.float32)

time: 155 us -> 160 us (1.032); the launches traced: 154 us -> 157 us
  starting transfers between devices: 51.3 us -> 66.4 us
  waiting for transfers between devices: 55.5 us -> 48.7 us
  other arithmetic: 14.1 us -> 10.1 us
  Pallas kernels: 13.8 us -> 11.3 us
    ppermute x15, starting transfers between devices: 20.2 us -> 33.4 us  [dp_shift(): return lax.ppermute(value, 'dp', pairs)]
    all_to_all x1, waiting for transfers between devices: 6.7 us -> 0.01 us  [step(): lax.all_to_all(embedded.reshape(shards, feature_cols, docs), 'dp', split_...]
    reduce_sum x3 -> x2, other arithmetic: 5.34 us -> 1.37 us  [the longest x1 1 us: step(): norms = jnp.sum(wide * wide, axis=0, keepdims=True)]
    all_to_all x1, starting transfers between devices: 8.39 us -> 12.1 us  [step(): lax.all_to_all(embedded.reshape(shards, feature_cols, docs), 'dp', split_...]
    ppermute x12, waiting for transfers between devices: 31.4 us -> 28.6 us  [mp_shift(): return lax.ppermute(value, 'mp', [(i, (i + step) % MP) for i in range(MP)])]
    ppermute x15, waiting for transfers between devices: 17.4 us -> 20.1 us  [dp_shift(): return lax.ppermute(value, 'dp', pairs)]
    pallas_call x1, Pallas kernels: 8.16 us -> 5.66 us  [new_state(): pl.pallas_call(sums_kernel, grid_spec=pltpu.PrefetchScalarGridSpec(num_sc...]
    another operation x1 -> x2, other arithmetic: 1.62 us -> 3.5 us  [gather_tables(): tables = [jnp.stack(upper), jnp.stack(lower)]]
  transfers between devices with their start and end apart: 28 -> 28, of which waited for: 13 -> 9; matrix products, arithmetic and copies ran while one was open for 20% -> 17% of each run, Pallas kernels for 4% -> 4%
where the time goes in v3:
time: 160 us; the launch traced here: 157 us
  starting transfers between devices  66.4 us (42%)
  waiting for transfers between devices  48.7 us (30%)
  matrix products  17.5 us (11%)
  Pallas kernels  11.3 us (7%)
  other arithmetic  10.1 us (6%)
  local copies, waits for them, and re-layouts  2.23 us (1%)
    ppermute x15, starting transfers between devices, dp_shift(): return lax.ppermute(value, 'dp', pairs)  33.4 us
    ppermute x12, waiting for transfers between devices, mp_shift(): return lax.ppermute(value, 'mp', [(i, (i + step) % MP) for i in range(MP)])  28.6 us
    ppermute x12, starting transfers between devices, mp_shift(): return lax.ppermute(value, 'mp', [(i, (i + step) % MP) for i in range(MP)])  20.9 us
    ppermute x15, waiting for transfers between devices, dp_shift(): return lax.ppermute(value, 'dp', pairs)  20.1 us
    all_to_all x1, starting transfers between devices, step(): lax.all_to_all(embedded.reshape(shards, feature_cols, docs), 'dp', split_...  12.1 us
    dot_general x4, matrix products, step(): lax.dot_general(part, rows, (((0,), (0,)), ((), ())), preferred_element_t...  9.03 us
    dot_general x4, matrix products, partial(): return jnp.dot(pooled, w, preferred_element_type=jnp.float32) * SCALE  8.42 us
    pallas_call x1, Pallas kernels, new_state(): pl.pallas_call(sums_kernel, grid_spec=pltpu.PrefetchScalarGridSpec(num_sc...  5.66 us
  transfers between devices with their start and end apart: 28, of which 9 were waited for; matrix products, arithmetic and copies ran while one was open for 17% of the time, Pallas kernels for 4%

profile of v3, /device:TPU:1, one launch (start us, length us, event | category | flops | bytes accessed | tf_op | source)
XLA Modules:
  0.0 157.3 jit_solution(3405053989848845642)
XLA Ops:
  2.5 2.5 %collective-permute-start.12 = (bf16[64,1024]{1,0:T(8,128)(2,1)S(1)}, bf16[64,1024]{1,0:T(8,128)(2,1)S(1)}, u32[]{:S(2)}, u32[]{:S(2)}) collective-permute-start(bf16[64,1024]{1,0:T(8,128)(2,1)S(1)} %concatenate.15), channel_id=1, source_target_pairs={{0,32},{4,36},{8,40},{12,44},{16,48},{20,52},{24,56},{28,60},{32,0... | collective-permute-start | bytes 393224 | tf_op jit(solution)/shard_map/ppermute | solution.py:42
  7.3 5.2 %collective-permute-start.1 = (f16[128,896]{0,1:T(8,128)(2,1)S(1)}, f16[128,896]{0,1:T(8,128)(2,1)S(1)}, u32[]{:S(2)}, u32[]{:S(2)}) collective-permute-start(f16[128,896]{0,1:T(8,128)(2,1)S(1)} %get-tuple-element.68), channel_id=1, source_target_pairs={{0,3},{1,0},{2,1},{3,2},{4,7},{5,4},{6,5},{7,6},{8,11},{9,8},{10,9... | collective-permute-start | bytes 688136 | tf_op jit(solution)/shard_map/ppermute | solution.py:18
  20.9 3.3 %collective-permute-done = f16[128,896]{0,1:T(8,128)(2,1)S(1)} collective-permute-done((f16[128,896]{0,1:T(8,128)(2,1)S(1)}, f16[128,896]{0,1:T(8,128)(2,1)S(1)}, u32[]{:S(2)}, u32[]{:S(2)}) %collective-permute-start) | collective-permute-done | bytes 229408 | tf_op jit(solution)/shard_map/ppermute | solution.py:18
  25.9 2.4 %collective-permute-start.14 = (bf16[2,32,1024]{2,1,0:T(8,128)(2,1)S(1)}, bf16[2,32,1024]{2,1,0:T(8,128)(2,1)S(1)}, u32[]{:S(2)}, u32[]{:S(2)}) collective-permute-start(bf16[2,32,1024]{2,1,0:T(8,128)(2,1)S(1)} %get-tuple-element.35), channel_id=1, source_target_pairs={{0,16},{4,20},{8,24},{12,28},{16,0},{20,4},{24,8},{28,12},{32,48},... | collective-permute-start | bytes 393224 | tf_op jit(solution)/shard_map/ppermute | solution.py:42
  29.5 3.6 %collective-permute-start.3 = (f16[128,896]{0,1:T(8,128)(2,1)S(1)}, f16[128,896]{0,1:T(8,128)(2,1)S(1)}, u32[]{:S(2)}, u32[]{:S(2)}) collective-permute-start(f16[128,896]{0,1:T(8,128)(2,1)S(1)} %slice_convert_fusion), channel_id=1, source_target_pairs={{0,3},{1,0},{2,1},{3,2},{4,7},{5,4},{6,5},{7,6},{8,11},{9,8},{10,9... | collective-permute-start | bytes 688136 | tf_op jit(solution)/shard_map/ppermute | solution.py:18
  33.0 3.6 %collective-permute-start.5 = (f16[128,896]{0,1:T(8,128)(2,1)S(1)}, f16[128,896]{0,1:T(8,128)(2,1)S(1)}, u32[]{:S(2)}, u32[]{:S(2)}) collective-permute-start(f16[128,896]{0,1:T(8,128)(2,1)S(1)} %fusion.61), channel_id=1, source_target_pairs={{0,3},{1,0},{2,1},{3,2},{4,7},{5,4},{6,5},{7,6},{8,11},{9,8},{10,9... | collective-permute-start | bytes 688136 | tf_op jit(solution)/shard_map/ppermute | solution.py:18
  38.0 2.8 %collective-permute-start.20 = (bf16[2,32,1024]{2,1,0:T(8,128)(2,1)S(1)}, bf16[2,32,1024]{2,1,0:T(8,128)(2,1)S(1)}, u32[]{:S(2)}, u32[]{:S(2)}) collective-permute-start(bf16[2,32,1024]{2,1,0:T(8,128)(2,1)S(1)} %get-tuple-element.39), channel_id=1, source_target_pairs={{0,128},{4,132},{8,136},{12,140},{16,144},{20,148},{24,152},{28,15... | collective-permute-start | bytes 393224 | tf_op jit(solution)/shard_map/ppermute | solution.py:42
  41.7 3.8 %collective-permute-done.2 = f16[128,896]{0,1:T(8,128)(2,1)S(1)} collective-permute-done((f16[128,896]{0,1:T(8,128)(2,1)S(1)}, f16[128,896]{0,1:T(8,128)(2,1)S(1)}, u32[]{:S(2)}, u32[]{:S(2)}) %collective-permute-start.2) | collective-permute-done | bytes 229408 | tf_op jit(solution)/shard_map/ppermute | solution.py:18
  46.7 2.7 %collective-permute-start.17 = (bf16[4,2,32,1024]{3,2,1,0:T(8,128)(2,1)S(1)}, bf16[4,2,32,1024]{3,2,1,0:T(8,128)(2,1)S(1)}, u32[]{:S(2)}, u32[]{:S(2)}) collective-permute-start(bf16[4,2,32,1024]{3,2,1,0:T(8,128)(2,1)S(1)} %pad_maximum_fusion.3), channel_id=1, source_target_pairs={{0,128},{4,132},{8,136},{12,140},{16,144},{20,148},{24,152},{28,15... | collective-permute-start | bytes 1572872 | tf_op jit(solution)/shard_map/ppermute | solution.py:42
  51.4 2.9 %collective-permute-start.6 = (f16[448,256]{1,0:T(8,128)(2,1)S(1)}, f16[448,256]{1,0:T(8,128)(2,1)S(1)}, u32[]{:S(2)}, u32[]{:S(2)}) collective-permute-start(f16[448,256]{1,0:T(8,128)(2,1)S(1)} %get-tuple-element.66), channel_id=1, source_target_pairs={{0,3},{1,0},{2,1},{3,2},{4,7},{5,4},{6,5},{7,6},{8,11},{9,8},{10,9... | collective-permute-start | bytes 688136 | tf_op jit(solution)/shard_map/ppermute | solution.py:18
  54.5 3.5 %collective-permute-done.8 = f16[448,256]{1,0:T(8,128)(2,1)S(1)} collective-permute-done((f16[448,256]{1,0:T(8,128)(2,1)S(1)}, f16[448,256]{1,0:T(8,128)(2,1)S(1)}, u32[]{:S(2)}, u32[]{:S(2)}) %collective-permute-start.8) | collective-permute-done | bytes 229408 | tf_op jit(solution)/shard_map/ppermute | solution.py:18
  60.7 3.5 %collective-permute-done.7 = f16[448,256]{1,0:T(8,128)(2,1)S(1)} collective-permute-done((f16[448,256]{1,0:T(8,128)(2,1)S(1)}, f16[448,256]{1,0:T(8,128)(2,1)S(1)}, u32[]{:S(2)}, u32[]{:S(2)}) %collective-permute-start.7) | collective-permute-done | bytes 229408 | tf_op jit(solution)/shard_map/ppermute | solution.py:18
  64.3 7.0 %collective-permute-done.11 = f16[448,256]{1,0:T(8,128)(2,1)S(1)} collective-permute-done((f16[448,256]{1,0:T(8,128)(2,1)S(1)}, f16[448,256]{1,0:T(8,128)(2,1)S(1)}, u32[]{:S(2)}, u32[]{:S(2)}) %collective-permute-start.11) | collective-permute-done | bytes 229408 | tf_op jit(solution)/shard_map/ppermute | solution.py:18
  71.4 2.5 %collective-permute-start.10 = (f16[448,256]{1,0:T(8,128)(2,1)S(1)}, f16[448,256]{1,0:T(8,128)(2,1)S(1)}, u32[]{:S(2)}, u32[]{:S(2)}) collective-permute-start(f16[448,256]{1,0:T(8,128)(2,1)S(1)} %collective-permute-done.7), channel_id=1, source_target_pairs={{0,3},{1,0},{2,1},{3,2},{4,7},{5,4},{6,5},{7,6},{8,11},{9,8},{10,9... | collective-permute-start | bytes 688136 | tf_op jit(solution)/shard_map/ppermute | solution.py:18
  75.1 5.5 %collective-permute-done.10 = f16[448,256]{1,0:T(8,128)(2,1)S(1)} collective-permute-done((f16[448,256]{1,0:T(8,128)(2,1)S(1)}, f16[448,256]{1,0:T(8,128)(2,1)S(1)}, u32[]{:S(2)}, u32[]{:S(2)}) %collective-permute-start.10) | collective-permute-done | bytes 229408 | tf_op jit(solution)/shard_map/ppermute | solution.py:18
  80.6 11.7 %collective-permute-start.23 = (bf16[4,2,32,1024]{3,2,1,0:T(8,128)(2,1)S(1)}, bf16[4,2,32,1024]{3,2,1,0:T(8,128)(2,1)}, u32[]{:S(2)}, u32[]{:S(2)}) collective-permute-start(bf16[4,2,32,1024]{3,2,1,0:T(8,128)(2,1)S(1)} %pad_maximum_fusion.4), channel_id=1, source_target_pairs={{0,16},{4,20},{8,24},{12,28},{16,0},{20,4},{24,8},{28,12},{32,48},... | collective-permute-start | bytes 1572872 | tf_op jit(solution)/shard_map/ppermute | solution.py:42
  95.4 12.1 %all-to-all-start = ((bf16[64,56,256]{2,1,0:T(8,128)(2,1)}), bf16[64,56,256]{2,1,0:T(8,128)(2,1)}, u32[]{:S(2)}, u32[]{:S(2)}) async-start(bf16[64,56,256]{2,1,0:T(8,128)(2,1)} %bitcast.5), calls=%async_computation | async-start | bytes 3670016 | tf_op jit(solution)/shard_map/all_to_all | solution.py:283
  108.1 3.8 %put_in_order.1 = (bf16[4096,256]{1,0:T(8,128)(2,1)}, f32[1,256]{1,0:T(1,128)}) custom-call(s32[128]{0:T(128)} %pad_add_fusion.blocks_ref, bf16[3584,256]{1,0:T(8,128)(2,1)} %put_in_place.1.whole_ref), custom_call_target="tpu_custom_call" | custom-call | flops 3000000 | bytes 3670016 | tf_op jit(solution)/shard_map/put_in_order/pallas_call | solution.py:136
  112.0 20.1 %collective-permute-done.22 = bf16[4,2,32,1024]{3,2,1,0:T(8,128)(2,1)} collective-permute-done((bf16[4,2,32,1024]{3,2,1,0:T(8,128)(2,1)S(1)}, bf16[4,2,32,1024]{3,2,1,0:T(8,128)(2,1)}, u32[]{:S(2)}, u32[]{:S(2)}) %collective-permute-start.22) | collective-permute-done | bytes 524320 | tf_op jit(solution)/shard_map/ppermute | solution.py:42
  134.0 3.8 %collective-permute-start.25 = (bf16[4,4,2,32,1024]{4,3,2,1,0:T(8,128)(2,1)S(1)}, bf16[4,4,2,32,1024]{4,3,2,1,0:T(8,128)(2,1)}, u32[]{:S(2)}, u32[]{:S(2)}) collective-permute-start(bf16[4,4,2,32,1024]{4,3,2,1,0:T(8,128)(2,1)S(1)} %pad_maximum_fusion), channel_id=1, source_target_pairs={{0,4},{4,0},{8,12},{12,8},{16,20},{20,16},{24,28},{28,24},{32,36},... | collective-permute-start | bytes 6291464 | tf_op jit(solution)/shard_map/ppermute | solution.py:42
  140.0 2.6 %fusion.43 = f32[256,1024]{1,0:T(8,128)S(1)} fusion(bf16[1024,1024]{1,0:T(8,128)(2,1)} %bitcast.29, bf16[4096,256]{1,0:T(8,128)(2,1)} %get-tuple-element.47), kind=kOutput, calls=%fused_computation.51 | convolution fusion | flops 536870912 | bytes 3670016 | tf_op jit(solution)/shard_map/dot_general | solution.py:297
  145.9 2.3 %fusion.39 = f32[256,1024]{1,0:T(8,128)S(1)} fusion(bf16[1024,1024]{1,0:T(8,128)(2,1)} %bitcast.32, bf16[4096,256]{1,0:T(8,128)(2,1)S(1)} %copy-done.1), kind=kOutput, calls=%fused_computation.47 | convolution fusion | flops 536870912 | bytes 3670016 | tf_op jit(solution)/shard_map/dot_general | solution.py:297
  148.3 3.4 %fusion.10 = f32[256,1024]{1,0:T(8,128)} fusion(f32[256,1024]{1,0:T(8,128)S(1)} %fusion.39, f32[256,1024]{1,0:T(8,128)S(1)} %convolution_add_fusion.1, bf16[1024,1024]{1,0:T(8,128)(2,1)} %bitcast.31, bf16[4096,256]{1,0:T(8,128)(2,1)S(1)} %copy-done.1, f32[1024]{0:T(1024)S(1)} %convert_reduce_fusion, f32[256]{0:T(256)S(1)} %bitcast.76), kind=kOutput, calls=%fused_computation.13 | convolution fusion | flops 538181632 | bytes 5772288 | tf_op jit(solution)/shard_map/dot_general | solution.py:297
  151.6 5.7 %new_state.1 = (f32[56,1024]{1,0:T(8,128)}, f32[1,1024]{1,0:T(1,128)}, bf16[56,1024]{1,0:T(8,128)(2,1)}) custom-call(s32[1]{0:T(128)} %bitcast.33.first_ref, s32[64]{0:T(128)} %fusion.82.entries_ref, bf16[64,8,1024]{2,1,0:T(8,128)(2,1)} %pad_maximum_fusion.2.codes_ref, bf16[64,56,256]{2,1,0:T(8,128)(2,1)} %all-to-all-done.cols_ref, f32[56,1024]{1,0:T(8,128)} %bitcast.68, ...), custom_call_target="tpu_custom_call" | custom-call | flops 1879048192 | bytes 1835008 | tf_op jit(solution)/shard_map/new_state/pallas_call | solution.py:195
  (107 shorter events, 35.8 us)
Async XLA Ops:
  2.5 21.8 %collective-permute-start.12 = (bf16[64,1024]{1,0:T(8,128)(2,1)S(1)}, bf16[64,1024]{1,0:T(8,128)(2,1)S(1)}, u32[]{:S(2)}, u32[]{:S(2)}) collective-permute-start(bf16[64,1024]{1,0:T(8,128)(2,1)S(1)} %concatenate.15), channel_id=1, source_target_pairs={{0,32},{4,36},{8,40},{12,44},{16,48},{20,52},{24,56},{28,60},{32,0... | collective-permute-start | bytes 393224 | tf_op jit(solution)/shard_map/ppermute | solution.py:42
  7.3 13.6 %collective-permute-start.1 = (f16[128,896]{0,1:T(8,128)(2,1)S(1)}, f16[128,896]{0,1:T(8,128)(2,1)S(1)}, u32[]{:S(2)}, u32[]{:S(2)}) collective-permute-start(f16[128,896]{0,1:T(8,128)(2,1)S(1)} %get-tuple-element.68), channel_id=1, source_target_pairs={{0,3},{1,0},{2,1},{3,2},{4,7},{5,4},{6,5},{7,6},{8,11},{9,8},{10,9... | collective-permute-start | bytes 688136 | tf_op jit(solution)/shard_map/ppermute | solution.py:18
  12.5 11.7 %collective-permute-start = (f16[128,896]{0,1:T(8,128)(2,1)S(1)}, f16[128,896]{0,1:T(8,128)(2,1)S(1)}, u32[]{:S(2)}, u32[]{:S(2)}) collective-permute-start(f16[128,896]{0,1:T(8,128)(2,1)S(1)} %get-tuple-element.69), channel_id=1, source_target_pairs={{0,1},{1,2},{2,3},{3,0},{4,5},{5,6},{6,7},{7,4},{8,9},{9,10},{10,1... | collective-permute-start | bytes 688136 | tf_op jit(solution)/shard_map/ppermute | solution.py:18
  24.4 8.7 %collective-permute-start.15 = (bf16[2,32,1024]{2,1,0:T(8,128)(2,1)S(1)}, bf16[2,32,1024]{2,1,0:T(8,128)(2,1)S(1)}, u32[]{:S(2)}, u32[]{:S(2)}) collective-permute-start(bf16[2,32,1024]{2,1,0:T(8,128)(2,1)S(1)} %get-tuple-element.35), channel_id=1, source_target_pairs={{0,8},{4,12},{8,16},{12,20},{16,24},{20,28},{24,0},{28,4},{32,40},... | collective-permute-start | bytes 393224 | tf_op jit(solution)/shard_map/ppermute | solution.py:42
  28.4 8.2 %collective-permute-start.13 = (bf16[2,32,1024]{2,1,0:T(8,128)(2,1)S(1)}, bf16[2,32,1024]{2,1,0:T(8,128)(2,1)S(1)}, u32[]{:S(2)}, u32[]{:S(2)}) collective-permute-start(bf16[2,32,1024]{2,1,0:T(8,128)(2,1)S(1)} %get-tuple-element.35), channel_id=1, source_target_pairs={{0,24},{4,28},{8,0},{12,4},{16,8},{20,12},{24,16},{28,20},{32,56},... | collective-permute-start | bytes 393224 | tf_op jit(solution)/shard_map/ppermute | solution.py:42
  29.5 8.5 %collective-permute-start.4 = (f16[128,896]{0,1:T(8,128)(2,1)S(1)}, f16[128,896]{0,1:T(8,128)(2,1)S(1)}, u32[]{:S(2)}, u32[]{:S(2)}) collective-permute-start(f16[128,896]{0,1:T(8,128)(2,1)S(1)} %copy-done.10), channel_id=1, source_target_pairs={{0,1},{1,2},{2,3},{3,0},{4,5},{5,6},{6,7},{7,4},{8,9},{9,10},{10,1... | collective-permute-start | bytes 688136 | tf_op jit(solution)/shard_map/ppermute | solution.py:18
  29.5 11.3 %collective-permute-start.3 = (f16[128,896]{0,1:T(8,128)(2,1)S(1)}, f16[128,896]{0,1:T(8,128)(2,1)S(1)}, u32[]{:S(2)}, u32[]{:S(2)}) collective-permute-start(f16[128,896]{0,1:T(8,128)(2,1)S(1)} %slice_convert_fusion), channel_id=1, source_target_pairs={{0,3},{1,0},{2,1},{3,2},{4,7},{5,4},{6,5},{7,6},{8,11},{9,8},{10,9... | collective-permute-start | bytes 688136 | tf_op jit(solution)/shard_map/ppermute | solution.py:18
  33.0 12.5 %collective-permute-start.2 = (f16[128,896]{0,1:T(8,128)(2,1)S(1)}, f16[128,896]{0,1:T(8,128)(2,1)S(1)}, u32[]{:S(2)}, u32[]{:S(2)}) collective-permute-start(f16[128,896]{0,1:T(8,128)(2,1)S(1)} %fusion.64), channel_id=1, source_target_pairs={{0,1},{1,2},{2,3},{3,0},{4,5},{5,6},{6,7},{7,4},{8,9},{9,10},{10,1... | collective-permute-start | bytes 688136 | tf_op jit(solution)/shard_map/ppermute | solution.py:18
  33.0 13.6 %collective-permute-start.5 = (f16[128,896]{0,1:T(8,128)(2,1)S(1)}, f16[128,896]{0,1:T(8,128)(2,1)S(1)}, u32[]{:S(2)}, u32[]{:S(2)}) collective-permute-start(f16[128,896]{0,1:T(8,128)(2,1)S(1)} %fusion.61), channel_id=1, source_target_pairs={{0,3},{1,0},{2,1},{3,2},{4,7},{5,4},{6,5},{7,6},{8,11},{9,8},{10,9... | collective-permute-start | bytes 688136 | tf_op jit(solution)/shard_map/ppermute | solution.py:18
  36.6 13.1 %collective-permute-start.21 = (bf16[2,32,1024]{2,1,0:T(8,128)(2,1)S(1)}, bf16[2,32,1024]{2,1,0:T(8,128)(2,1)S(1)}, u32[]{:S(2)}, u32[]{:S(2)}) collective-permute-start(bf16[2,32,1024]{2,1,0:T(8,128)(2,1)S(1)} %get-tuple-element.39), channel_id=1, source_target_pairs={{0,64},{4,68},{8,72},{12,76},{16,80},{20,84},{24,88},{28,92},{32,9... | collective-permute-start | bytes 393224 | tf_op jit(solution)/shard_map/ppermute | solution.py:42
  38.0 12.8 %collective-permute-start.20 = (bf16[2,32,1024]{2,1,0:T(8,128)(2,1)S(1)}, bf16[2,32,1024]{2,1,0:T(8,128)(2,1)S(1)}, u32[]{:S(2)}, u32[]{:S(2)}) collective-permute-start(bf16[2,32,1024]{2,1,0:T(8,128)(2,1)S(1)} %get-tuple-element.39), channel_id=1, source_target_pairs={{0,128},{4,132},{8,136},{12,140},{16,144},{20,148},{24,152},{28,15... | collective-permute-start | bytes 393224 | tf_op jit(solution)/shard_map/ppermute | solution.py:42
  40.8 10.7 %collective-permute-start.19 = (bf16[2,32,1024]{2,1,0:T(8,128)(2,1)S(1)}, bf16[2,32,1024]{2,1,0:T(8,128)(2,1)S(1)}, u32[]{:S(2)}, u32[]{:S(2)}) collective-permute-start(bf16[2,32,1024]{2,1,0:T(8,128)(2,1)S(1)} %get-tuple-element.39), channel_id=1, source_target_pairs={{0,192},{4,196},{8,200},{12,204},{16,208},{20,212},{24,216},{28,22... | collective-permute-start | bytes 393224 | tf_op jit(solution)/shard_map/ppermute | solution.py:42
  45.5 46.9 %collective-permute-start.18 = (bf16[4,2,32,1024]{3,2,1,0:T(8,128)(2,1)S(1)}, bf16[4,2,32,1024]{3,2,1,0:T(8,128)(2,1)S(1)}, u32[]{:S(2)}, u32[]{:S(2)}) collective-permute-start(bf16[4,2,32,1024]{3,2,1,0:T(8,128)(2,1)S(1)} %pad_maximum_fusion.3), channel_id=1, source_target_pairs={{0,64},{4,68},{8,72},{12,76},{16,80},{20,84},{24,88},{28,92},{32,9... | collective-permute-start | bytes 1572872 | tf_op jit(solution)/shard_map/ppermute | solution.py:42
  46.7 65.2 %collective-permute-start.17 = (bf16[4,2,32,1024]{3,2,1,0:T(8,128)(2,1)S(1)}, bf16[4,2,32,1024]{3,2,1,0:T(8,128)(2,1)S(1)}, u32[]{:S(2)}, u32[]{:S(2)}) collective-permute-start(bf16[4,2,32,1024]{3,2,1,0:T(8,128)(2,1)S(1)} %pad_maximum_fusion.3), channel_id=1, source_target_pairs={{0,128},{4,132},{8,136},{12,140},{16,144},{20,148},{24,152},{28,15... | collective-permute-start | bytes 1572872 | tf_op jit(solution)/shard_map/ppermute | solution.py:42
  49.8 62.1 %collective-permute-start.16 = (bf16[4,2,32,1024]{3,2,1,0:T(8,128)(2,1)S(1)}, bf16[4,2,32,1024]{3,2,1,0:T(8,128)(2,1)S(1)}, u32[]{:S(2)}, u32[]{:S(2)}) collective-permute-start(bf16[4,2,32,1024]{3,2,1,0:T(8,128)(2,1)S(1)} %pad_maximum_fusion.3), channel_id=1, source_target_pairs={{0,192},{4,196},{8,200},{12,204},{16,208},{20,212},{24,216},{28,22... | collective-permute-start | bytes 1572872 | tf_op jit(solution)/shard_map/ppermute | solution.py:42
  59.3 12.1 %collective-permute-start.11 = (f16[448,256]{1,0:T(8,128)(2,1)S(1)}, f16[448,256]{1,0:T(8,128)(2,1)S(1)}, u32[]{:S(2)}, u32[]{:S(2)}) collective-permute-start(f16[448,256]{1,0:T(8,128)(2,1)S(1)} %get-tuple-element.67), channel_id=1, source_target_pairs={{0,1},{1,2},{2,3},{3,0},{4,5},{5,6},{6,7},{7,4},{8,9},{9,10},{10,1... | collective-permute-start | bytes 688136 | tf_op jit(solution)/shard_map/ppermute | solution.py:18
  64.2 10.4 %collective-permute-start.9 = (f16[448,256]{1,0:T(8,128)(2,1)S(1)}, f16[448,256]{1,0:T(8,128)(2,1)S(1)}, u32[]{:S(2)}, u32[]{:S(2)}) collective-permute-start(f16[448,256]{1,0:T(8,128)(2,1)S(1)} %collective-permute-done.8), channel_id=1, source_target_pairs={{0,1},{1,2},{2,3},{3,0},{4,5},{5,6},{6,7},{7,4},{8,9},{9,10},{10,1... | collective-permute-start | bytes 688136 | tf_op jit(solution)/shard_map/ppermute | solution.py:18
  71.4 9.2 %collective-permute-start.10 = (f16[448,256]{1,0:T(8,128)(2,1)S(1)}, f16[448,256]{1,0:T(8,128)(2,1)S(1)}, u32[]{:S(2)}, u32[]{:S(2)}) collective-permute-start(f16[448,256]{1,0:T(8,128)(2,1)S(1)} %collective-permute-done.7), channel_id=1, source_target_pairs={{0,3},{1,0},{2,1},{3,2},{4,7},{5,4},{6,5},{7,6},{8,11},{9,8},{10,9... | collective-permute-start | bytes 688136 | tf_op jit(solution)/shard_map/ppermute | solution.py:18
  74.6 37.3 %collective-permute-start.24 = (bf16[4,2,32,1024]{3,2,1,0:T(8,128)(2,1)S(1)}, bf16[4,2,32,1024]{3,2,1,0:T(8,128)(2,1)S(1)}, u32[]{:S(2)}, u32[]{:S(2)}) collective-permute-start(bf16[4,2,32,1024]{3,2,1,0:T(8,128)(2,1)S(1)} %pad_maximum_fusion.4), channel_id=1, source_target_pairs={{0,8},{4,12},{8,16},{12,20},{16,24},{20,28},{24,0},{28,4},{32,40},... | collective-permute-start | bytes 1572872 | tf_op jit(solution)/shard_map/ppermute | solution.py:42
  80.6 31.4 %collective-permute-start.23 = (bf16[4,2,32,1024]{3,2,1,0:T(8,128)(2,1)S(1)}, bf16[4,2,32,1024]{3,2,1,0:T(8,128)(2,1)}, u32[]{:S(2)}, u32[]{:S(2)}) collective-permute-start(bf16[4,2,32,1024]{3,2,1,0:T(8,128)(2,1)S(1)} %pad_maximum_fusion.4), channel_id=1, source_target_pairs={{0,16},{4,20},{8,24},{12,28},{16,0},{20,4},{24,8},{28,12},{32,48},... | collective-permute-start | bytes 1572872 | tf_op jit(solution)/shard_map/ppermute | solution.py:42
  93.2 38.8 %collective-permute-start.22 = (bf16[4,2,32,1024]{3,2,1,0:T(8,128)(2,1)S(1)}, bf16[4,2,32,1024]{3,2,1,0:T(8,128)(2,1)}, u32[]{:S(2)}, u32[]{:S(2)}) collective-permute-start(bf16[4,2,32,1024]{3,2,1,0:T(8,128)(2,1)S(1)} %pad_maximum_fusion.4), channel_id=1, source_target_pairs={{0,24},{4,28},{8,0},{12,4},{16,8},{20,12},{24,16},{28,20},{32,56},... | collective-permute-start | bytes 1572872 | tf_op jit(solution)/shard_map/ppermute | solution.py:42
  95.4 56.2 %all-to-all-start = ((bf16[64,56,256]{2,1,0:T(8,128)(2,1)}), bf16[64,56,256]{2,1,0:T(8,128)(2,1)}, u32[]{:S(2)}, u32[]{:S(2)}) async-start(bf16[64,56,256]{2,1,0:T(8,128)(2,1)} %bitcast.5), calls=%async_computation | async-start | bytes 3670016 | tf_op jit(solution)/shard_map/all_to_all | solution.py:283
  134.0 9.4 %collective-permute-start.25 = (bf16[4,4,2,32,1024]{4,3,2,1,0:T(8,128)(2,1)S(1)}, bf16[4,4,2,32,1024]{4,3,2,1,0:T(8,128)(2,1)}, u32[]{:S(2)}, u32[]{:S(2)}) collective-permute-start(bf16[4,4,2,32,1024]{4,3,2,1,0:T(8,128)(2,1)S(1)} %pad_maximum_fusion), channel_id=1, source_target_pairs={{0,4},{4,0},{8,12},{12,8},{16,20},{20,16},{24,28},{28,24},{32,36},... | collective-permute-start | bytes 6291464 | tf_op jit(solution)/shard_map/ppermute | solution.py:42
  139.4 8.8 %collective-permute-start.26 = (bf16[4,4,2,32,1024]{4,3,2,1,0:T(8,128)(2,1)}, bf16[4,4,2,32,1024]{4,3,2,1,0:T(8,128)(2,1)}, u32[]{:S(2)}, u32[]{:S(2)}) collective-permute-start(bf16[4,4,2,32,1024]{4,3,2,1,0:T(8,128)(2,1)} %pad_maximum_fusion.1), channel_id=1, source_target_pairs={{0,4},{4,0},{8,12},{12,8},{16,20},{20,16},{24,28},{28,24},{32,36},... | collective-permute-start | bytes 6291464 | tf_op jit(solution)/shard_map/ppermute | solution.py:42
  (16 other events, 165.3 us)

commit v4 on v3

--- a/solution.py
+++ b/solution.py
@@ -49,13 +49,12 @@
 def first_lines(piece, hold):
     half = piece.shape[0] // 2
     pair = jnp.stack([piece, after(dp_shift(piece, 1, 1), hold)])
-    upper = shifts(pair[:, :half], 2)
-    lower = shifts(pair[:, half:], 0)
-    return upper, lower
-
-
-def second_lines(line, dim, hold):
-    return shifts(jnp.stack(after(line, hold)), dim)
+    return shifts(pair[:, :half], 2), shifts(pair[:, half:], 0)
+
+
+def second_lines(upper, lower, hold):
+    upper, lower = after((upper, lower), hold)
+    return shifts(jnp.stack(upper), 0), shifts(jnp.stack(lower), 2)
 
 
 def gather_tables(upper, lower, hold):
@@ -235,6 +234,11 @@
     far = partial(2).astype(f16)
     up = mp_shift(far[:half_docs], 1)
     down = mp_shift(far[half_docs:], -1)
+    ahead, behind = partial(1), partial(-1)
+    low_a, top_b = ahead[half_docs:].astype(f16), behind[:half_docs].astype(f16)
+    near = (low_a, top_b)
+    low_a, top_b = mp_shift(low_a, 1), mp_shift(top_b, -1)
+    ema_sums, assignments = after((ema_sums, assignments), near)
     sums_t = ema_sums.T
     centers = (sums_t / ema_counts[None, :]).astype(jnp.bfloat16)
     pair = jnp.stack([assignments // 64, assignments % 64]).astype(jnp.bfloat16).reshape(1, 2 * docs)
@@ -247,23 +251,18 @@
         norms = norms - coarse
     extra.append(jnp.zeros((4, width), jnp.bfloat16))
     centers = jnp.concatenate([centers] + extra)
-    ahead, behind = partial(1), partial(-1)
-    low_a, top_b = ahead[half_docs:].astype(f16), behind[:half_docs].astype(f16)
-    near = (low_a, top_b)
-    low_a, top_b = mp_shift(low_a, 1), mp_shift(top_b, -1)
     mine = partial(0)
     up, down = after((up, down), near, mine)
     top_a = (ahead[:half_docs] + up.astype(jnp.float32)).astype(f16)
     low_b = (behind[half_docs:] + down.astype(jnp.float32)).astype(f16)
     hold = (top_a, low_b)
     top_a, low_b = mp_shift(top_a, 1), mp_shift(low_b, -1)
-    upper, lower = first_lines(centers, hold)
-    upper = second_lines(upper, 0, hold)
+    lines = first_lines(centers, hold)
     top = mine[:half_docs] + top_a.astype(jnp.float32) + top_b.astype(jnp.float32)
     low = mine[half_docs:] + low_a.astype(jnp.float32) + low_b.astype(jnp.float32)
     share = jnp.concatenate([top, low]).T.astype(f16)
     first_half, second_half = share[:half], share[half:]
-    lower = second_lines(lower, 2, (first_half, second_half))
+    lines = second_lines(*lines, (first_half, second_half))
     a_first = mp_shift(first_half, 1)
     b_second = mp_shift(second_half, -1)
     a_second = mp_shift(second_half, 1)
@@ -284,7 +283,7 @@
         embedded.reshape(shards, feature_cols, docs), "dp", split_axis=0, concat_axis=0, tiled=True
     )
     ordered, doc_norms = put_in_order(blocks, embedded)
-    tables = gather_tables(upper, lower, doc_norms)
+    tables = gather_tables(*lines, doc_norms)
     upper = (feature_cols + 8) // 2
     tables = [t.reshape(shards // 2, upper, width) for t in tables]
     real = feature_cols - upper

time: 160 us -> 151 us (0.944); the launches traced: 157 us -> 150 us
  waiting for transfers between devices: 48.7 us -> 37.5 us
  other arithmetic: 10.1 us -> 13 us
    ppermute x12, waiting for transfers between devices: 28.6 us -> 16.5 us  [mp_shift(): return lax.ppermute(value, 'mp', [(i, (i + step) % MP) for i in range(MP)])]
    ppermute x12, starting transfers between devices: 20.9 us -> 25.8 us  [mp_shift(): return lax.ppermute(value, 'mp', [(i, (i + step) % MP) for i in range(MP)])]
    ppermute x15, starting transfers between devices: 33.4 us -> 30.7 us  [dp_shift(): return lax.ppermute(value, 'dp', pairs)]
    all_to_all x1, starting transfers between devices: 12.1 us -> 10.1 us  [step(): lax.all_to_all(embedded.reshape(shards, feature_cols, docs), 'dp', split_...]
  transfers between devices with their start and end apart: 28 -> 28, of which waited for: 9 -> 8; matrix products, arithmetic and copies ran while one was open for 17% -> 20% of each run, Pallas kernels for 4% -> 4%
where the time goes in v4:
time: 151 us; the launch traced here: 150 us
  starting transfers between devices  66.6 us (44%)
  waiting for transfers between devices  37.5 us (25%)
  matrix products  17.4 us (12%)
  other arithmetic  13 us (9%)
  Pallas kernels  11.3 us (7%)
  local copies, waits for them, and re-layouts  3.11 us (2%)
    ppermute x15, starting transfers between devices, dp_shift(): return lax.ppermute(value, 'dp', pairs)  30.7 us
    ppermute x12, starting transfers between devices, mp_shift(): return lax.ppermute(value, 'mp', [(i, (i + step) % MP) for i in range(MP)])  25.8 us
    ppermute x15, waiting for transfers between devices, dp_shift(): return lax.ppermute(value, 'dp', pairs)  21 us
    ppermute x12, waiting for transfers between devices, mp_shift(): return lax.ppermute(value, 'mp', [(i, (i + step) % MP) for i in range(MP)])  16.5 us
    all_to_all x1, starting transfers between devices, step(): lax.all_to_all(embedded.reshape(shards, feature_cols, docs), 'dp', split_...  10.1 us
    dot_general x4, matrix products, step(): lax.dot_general(part, rows, (((0,), (0,)), ((), ())), preferred_element_t...  9.03 us
    dot_general x4, matrix products, partial(): return jnp.dot(pooled, w, preferred_element_type=jnp.float32) * SCALE  8.42 us
    pallas_call x1, Pallas kernels, new_state(): pl.pallas_call(sums_kernel, grid_spec=pltpu.PrefetchScalarGridSpec(num_sc...  5.66 us
  transfers between devices with their start and end apart: 28, of which 8 were waited for; matrix products, arithmetic and copies ran while one was open for 20% of the time, Pallas kernels for 4%

profile of v4, /device:TPU:1, one launch (start us, length us, event | category | flops | bytes accessed | tf_op | source)
XLA Modules:
  0.0 150.1 jit_solution(12213150158289886367)
XLA Ops:
  4.5 6.8 %collective-permute-start.1 = (f16[128,896]{0,1:T(8,128)(2,1)}, f16[128,896]{0,1:T(8,128)(2,1)S(1)}, u32[]{:S(2)}, u32[]{:S(2)}) collective-permute-start(f16[128,896]{0,1:T(8,128)(2,1)} %get-tuple-element.72), channel_id=1, source_target_pairs={{0,3},{1,0},{2,1},{3,2},{4,7},{5,4},{6,5},{7,6},{8,11},{9,8},{10,9... | collective-permute-start | bytes 688136 | tf_op jit(solution)/shard_map/ppermute | solution.py:18
  18.2 2.4 %collective-permute-start.3 = (f16[128,896]{0,1:T(8,128)(2,1)}, f16[128,896]{0,1:T(8,128)(2,1)S(1)}, u32[]{:S(2)}, u32[]{:S(2)}) collective-permute-start(f16[128,896]{0,1:T(8,128)(2,1)} %slice_convert_fusion), channel_id=1, source_target_pairs={{0,3},{1,0},{2,1},{3,2},{4,7},{5,4},{6,5},{7,6},{8,11},{9,8},{10,9... | collective-permute-start | bytes 688136 | tf_op jit(solution)/shard_map/ppermute | solution.py:18
  26.1 3.4 %collective-permute-start.5 = (f16[128,896]{0,1:T(8,128)(2,1)S(1)}, f16[128,896]{0,1:T(8,128)(2,1)S(1)}, u32[]{:S(2)}, u32[]{:S(2)}) collective-permute-start(f16[128,896]{0,1:T(8,128)(2,1)S(1)} %fusion.61), channel_id=1, source_target_pairs={{0,3},{1,0},{2,1},{3,2},{4,7},{5,4},{6,5},{7,6},{8,11},{9,8},{10,9... | collective-permute-start | bytes 688136 | tf_op jit(solution)/shard_map/ppermute | solution.py:18
  29.5 9.4 %collective-permute-done.12 = bf16[64,1024]{1,0:T(8,128)(2,1)} collective-permute-done((bf16[64,1024]{1,0:T(8,128)(2,1)S(1)}, bf16[64,1024]{1,0:T(8,128)(2,1)}, u32[]{:S(2)}, u32[]{:S(2)}) %collective-permute-start.12) | collective-permute-done | bytes 131104 | tf_op jit(solution)/shard_map/ppermute | solution.py:42
  41.1 2.5 %collective-permute-start.17 = (bf16[2,32,1024]{2,1,0:T(8,128)(2,1)S(1)}, bf16[2,32,1024]{2,1,0:T(8,128)(2,1)S(1)}, u32[]{:S(2)}, u32[]{:S(2)}) collective-permute-start(bf16[2,32,1024]{2,1,0:T(8,128)(2,1)S(1)} %get-tuple-element.43), channel_id=1, source_target_pairs={{0,128},{4,132},{8,136},{12,140},{16,144},{20,148},{24,152},{28,15... | collective-permute-start | bytes 393224 | tf_op jit(solution)/shard_map/ppermute | solution.py:42
  48.0 2.6 %collective-permute-start.14 = (bf16[2,32,1024]{2,1,0:T(8,128)(2,1)S(1)}, bf16[2,32,1024]{2,1,0:T(8,128)(2,1)S(1)}, u32[]{:S(2)}, u32[]{:S(2)}) collective-permute-start(bf16[2,32,1024]{2,1,0:T(8,128)(2,1)S(1)} %get-tuple-element.39), channel_id=1, source_target_pairs={{0,16},{4,20},{8,24},{12,28},{16,0},{20,4},{24,8},{28,12},{32,48},... | collective-permute-start | bytes 393224 | tf_op jit(solution)/shard_map/ppermute | solution.py:42
  52.5 3.6 %collective-permute-start.6 = (f16[448,256]{1,0:T(8,128)(2,1)S(1)}, f16[448,256]{1,0:T(8,128)(2,1)S(1)}, u32[]{:S(2)}, u32[]{:S(2)}) collective-permute-start(f16[448,256]{1,0:T(8,128)(2,1)S(1)} %get-tuple-element.70), channel_id=1, source_target_pairs={{0,3},{1,0},{2,1},{3,2},{4,7},{5,4},{6,5},{7,6},{8,11},{9,8},{10,9... | collective-permute-start | bytes 688136 | tf_op jit(solution)/shard_map/ppermute | solution.py:18
  56.1 3.6 %collective-permute-start.7 = (f16[448,256]{1,0:T(8,128)(2,1)S(1)}, f16[448,256]{1,0:T(8,128)(2,1)S(1)}, u32[]{:S(2)}, u32[]{:S(2)}) collective-permute-start(f16[448,256]{1,0:T(8,128)(2,1)S(1)} %get-tuple-element.71), channel_id=1, source_target_pairs={{0,3},{1,0},{2,1},{3,2},{4,7},{5,4},{6,5},{7,6},{8,11},{9,8},{10,9... | collective-permute-start | bytes 688136 | tf_op jit(solution)/shard_map/ppermute | solution.py:18
  60.4 3.5 %collective-permute-done.8 = f16[448,256]{1,0:T(8,128)(2,1)S(1)} collective-permute-done((f16[448,256]{1,0:T(8,128)(2,1)S(1)}, f16[448,256]{1,0:T(8,128)(2,1)S(1)}, u32[]{:S(2)}, u32[]{:S(2)}) %collective-permute-start.8) | collective-permute-done | bytes 229408 | tf_op jit(solution)/shard_map/ppermute | solution.py:18
  64.0 5.1 %collective-permute-start.23 = (bf16[4,2,32,1024]{3,2,1,0:T(8,128)(2,1)S(1)}, bf16[4,2,32,1024]{3,2,1,0:T(8,128)(2,1)S(1)}, u32[]{:S(2)}, u32[]{:S(2)}) collective-permute-start(bf16[4,2,32,1024]{3,2,1,0:T(8,128)(2,1)S(1)} %pad_maximum_fusion.4), channel_id=1, source_target_pairs={{0,16},{4,20},{8,24},{12,28},{16,0},{20,4},{24,8},{28,12},{32,48},... | collective-permute-start | bytes 1572872 | tf_op jit(solution)/shard_map/ppermute | solution.py:42
  69.3 5.3 %collective-permute-done.7 = f16[448,256]{1,0:T(8,128)(2,1)S(1)} collective-permute-done((f16[448,256]{1,0:T(8,128)(2,1)S(1)}, f16[448,256]{1,0:T(8,128)(2,1)S(1)}, u32[]{:S(2)}, u32[]{:S(2)}) %collective-permute-start.7) | collective-permute-done | bytes 229408 | tf_op jit(solution)/shard_map/ppermute | solution.py:18
  76.6 2.6 %collective-permute-start.10 = (f16[448,256]{1,0:T(8,128)(2,1)S(1)}, f16[448,256]{1,0:T(8,128)(2,1)S(1)}, u32[]{:S(2)}, u32[]{:S(2)}) collective-permute-start(f16[448,256]{1,0:T(8,128)(2,1)S(1)} %collective-permute-done.7), channel_id=1, source_target_pairs={{0,3},{1,0},{2,1},{3,2},{4,7},{5,4},{6,5},{7,6},{8,11},{9,8},{10,9... | collective-permute-start | bytes 688136 | tf_op jit(solution)/shard_map/ppermute | solution.py:18
  79.3 3.8 %collective-permute-done.9 = f16[448,256]{1,0:T(8,128)(2,1)S(1)} collective-permute-done((f16[448,256]{1,0:T(8,128)(2,1)S(1)}, f16[448,256]{1,0:T(8,128)(2,1)S(1)}, u32[]{:S(2)}, u32[]{:S(2)}) %collective-permute-start.9) | collective-permute-done | bytes 229408 | tf_op jit(solution)/shard_map/ppermute | solution.py:18
  85.2 4.0 %collective-permute-start.20 = (bf16[4,2,32,1024]{3,2,1,0:T(8,128)(2,1)S(1)}, bf16[4,2,32,1024]{3,2,1,0:T(8,128)(2,1)}, u32[]{:S(2)}, u32[]{:S(2)}) collective-permute-start(bf16[4,2,32,1024]{3,2,1,0:T(8,128)(2,1)S(1)} %pad_maximum_fusion.3), channel_id=1, source_target_pairs={{0,128},{4,132},{8,136},{12,140},{16,144},{20,148},{24,152},{28,15... | collective-permute-start | bytes 1572872 | tf_op jit(solution)/shard_map/ppermute | solution.py:42
  92.5 10.1 %all-to-all-start = ((bf16[64,56,256]{2,1,0:T(8,128)(2,1)}), bf16[64,56,256]{2,1,0:T(8,128)(2,1)}, u32[]{:S(2)}, u32[]{:S(2)}) async-start(bf16[64,56,256]{2,1,0:T(8,128)(2,1)} %bitcast.5), calls=%async_computation | async-start | bytes 3670016 | tf_op jit(solution)/shard_map/all_to_all | solution.py:282
  103.3 3.8 %put_in_order.1 = (bf16[4096,256]{1,0:T(8,128)(2,1)}, f32[1,256]{1,0:T(1,128)}) custom-call(s32[128]{0:T(128)} %pad_add_fusion.blocks_ref, bf16[3584,256]{1,0:T(8,128)(2,1)} %put_in_place.1.whole_ref), custom_call_target="tpu_custom_call" | custom-call | flops 3000000 | bytes 3670016 | tf_op jit(solution)/shard_map/put_in_order/pallas_call | solution.py:135
  107.1 6.8 %collective-permute-done.20 = bf16[4,2,32,1024]{3,2,1,0:T(8,128)(2,1)} collective-permute-done((bf16[4,2,32,1024]{3,2,1,0:T(8,128)(2,1)S(1)}, bf16[4,2,32,1024]{3,2,1,0:T(8,128)(2,1)}, u32[]{:S(2)}, u32[]{:S(2)}) %collective-permute-start.20) | collective-permute-done | bytes 524320 | tf_op jit(solution)/shard_map/ppermute | solution.py:42
  113.9 4.8 %collective-permute-done.19 = bf16[4,2,32,1024]{3,2,1,0:T(8,128)(2,1)} collective-permute-done((bf16[4,2,32,1024]{3,2,1,0:T(8,128)(2,1)S(1)}, bf16[4,2,32,1024]{3,2,1,0:T(8,128)(2,1)}, u32[]{:S(2)}, u32[]{:S(2)}) %collective-permute-start.19) | collective-permute-done | bytes 524320 | tf_op jit(solution)/shard_map/ppermute | solution.py:42
  120.4 8.9 %collective-permute-start.25 = (bf16[4,4,2,32,1024]{4,3,2,1,0:T(8,128)(2,1)S(1)}, bf16[4,4,2,32,1024]{4,3,2,1,0:T(8,128)(2,1)}, u32[]{:S(2)}, u32[]{:S(2)}) collective-permute-start(bf16[4,4,2,32,1024]{4,3,2,1,0:T(8,128)(2,1)S(1)} %pad_maximum_fusion), channel_id=1, source_target_pairs={{0,4},{4,0},{8,12},{12,8},{16,20},{20,16},{24,28},{28,24},{32,36},... | collective-permute-start | bytes 6291464 | tf_op jit(solution)/shard_map/ppermute | solution.py:42
  129.3 3.0 %pad_maximum_fusion.1 = bf16[4,4,2,32,1024]{4,3,2,1,0:T(8,128)(2,1)} fusion(bf16[1,4,2,32,1024]{4,3,2,1,0:T(8,128)(2,1)} %bitcast.28, bf16[1,4,2,32,1024]{4,3,2,1,0:T(8,128)(2,1)} %bitcast.27, bf16[1,4,2,32,1024]{4,3,2,1,0:T(8,128)(2,1)} %bitcast.26, bf16[1,4,2,32,1024]{4,3,2,1,0:T(8,128)(2,1)S(1)} %bitcast.60), kind=kLoop, calls=%fused_computation.1 | loop fusion | flops 3145728 | bytes 4194304 | tf_op jit(solution)/shard_map/stack | solution.py:62
  132.8 2.6 %fusion.43 = f32[256,1024]{1,0:T(8,128)S(1)} fusion(bf16[1024,1024]{1,0:T(8,128)(2,1)} %bitcast.29, bf16[4096,256]{1,0:T(8,128)(2,1)} %get-tuple-element.51), kind=kOutput, calls=%fused_computation.51 | convolution fusion | flops 536870912 | bytes 3670016 | tf_op jit(solution)/shard_map/dot_general | solution.py:296
  138.7 2.3 %fusion.39 = f32[256,1024]{1,0:T(8,128)S(1)} fusion(bf16[1024,1024]{1,0:T(8,128)(2,1)} %bitcast.32, bf16[4096,256]{1,0:T(8,128)(2,1)S(1)} %copy-done.1), kind=kOutput, calls=%fused_computation.47 | convolution fusion | flops 536870912 | bytes 3670016 | tf_op jit(solution)/shard_map/dot_general | solution.py:296
  141.1 3.4 %fusion.10 = f32[256,1024]{1,0:T(8,128)} fusion(f32[256,1024]{1,0:T(8,128)S(1)} %fusion.39, f32[256,1024]{1,0:T(8,128)S(1)} %convolution_add_fusion.1, bf16[1024,1024]{1,0:T(8,128)(2,1)} %bitcast.31, bf16[4096,256]{1,0:T(8,128)(2,1)S(1)} %copy-done.1, f32[1024]{0:T(1024)S(1)} %convert_reduce_fusion, f32[256]{0:T(256)S(1)} %bitcast.74), kind=kOutput, calls=%fused_computation.13 | convolution fusion | flops 538181632 | bytes 5772288 | tf_op jit(solution)/shard_map/dot_general | solution.py:296
  144.5 5.7 %new_state.1 = (f32[56,1024]{1,0:T(8,128)}, f32[1,1024]{1,0:T(1,128)}, bf16[56,1024]{1,0:T(8,128)(2,1)}) custom-call(s32[1]{0:T(128)} %bitcast.33.first_ref, s32[64]{0:T(128)} %fusion.82.entries_ref, bf16[64,8,1024]{2,1,0:T(8,128)(2,1)} %pad_maximum_fusion.2.codes_ref, bf16[64,56,256]{2,1,0:T(8,128)(2,1)} %all-to-all-done.cols_ref, f32[56,1024]{1,0:T(8,128)} %bitcast.67, ...), custom_call_target="tpu_custom_call" | custom-call | flops 1879048192 | bytes 1835008 | tf_op jit(solution)/shard_map/new_state/pallas_call | solution.py:194
  (103 shorter events, 39.3 us)
Async XLA Ops:
  4.5 20.2 %collective-permute-start.1 = (f16[128,896]{0,1:T(8,128)(2,1)}, f16[128,896]{0,1:T(8,128)(2,1)S(1)}, u32[]{:S(2)}, u32[]{:S(2)}) collective-permute-start(f16[128,896]{0,1:T(8,128)(2,1)} %get-tuple-element.72), channel_id=1, source_target_pairs={{0,3},{1,0},{2,1},{3,2},{4,7},{5,4},{6,5},{7,6},{8,11},{9,8},{10,9... | collective-permute-start | bytes 688136 | tf_op jit(solution)/shard_map/ppermute | solution.py:18
  11.4 13.4 %collective-permute-start = (f16[128,896]{0,1:T(8,128)(2,1)S(1)}, f16[128,896]{0,1:T(8,128)(2,1)}, u32[]{:S(2)}, u32[]{:S(2)}) collective-permute-start(f16[128,896]{0,1:T(8,128)(2,1)S(1)} %get-tuple-element.73), channel_id=1, source_target_pairs={{0,1},{1,2},{2,3},{3,0},{4,5},{5,6},{6,7},{7,4},{8,9},{9,10},{10,1... | collective-permute-start | bytes 688136 | tf_op jit(solution)/shard_map/ppermute | solution.py:18
  14.2 26.8 %collective-permute-start.4 = (f16[128,896]{0,1:T(8,128)(2,1)}, f16[128,896]{0,1:T(8,128)(2,1)S(1)}, u32[]{:S(2)}, u32[]{:S(2)}) collective-permute-start(f16[128,896]{0,1:T(8,128)(2,1)} %slice_convert_fusion.1), channel_id=1, source_target_pairs={{0,1},{1,2},{2,3},{3,0},{4,5},{5,6},{6,7},{7,4},{8,9},{9,10},{10,1... | collective-permute-start | bytes 688136 | tf_op jit(solution)/shard_map/ppermute | solution.py:18
  18.2 25.3 %collective-permute-start.3 = (f16[128,896]{0,1:T(8,128)(2,1)}, f16[128,896]{0,1:T(8,128)(2,1)S(1)}, u32[]{:S(2)}, u32[]{:S(2)}) collective-permute-start(f16[128,896]{0,1:T(8,128)(2,1)} %slice_convert_fusion), channel_id=1, source_target_pairs={{0,3},{1,0},{2,1},{3,2},{4,7},{5,4},{6,5},{7,6},{8,11},{9,8},{10,9... | collective-permute-start | bytes 688136 | tf_op jit(solution)/shard_map/ppermute | solution.py:18
  21.8 17.1 %collective-permute-start.12 = (bf16[64,1024]{1,0:T(8,128)(2,1)S(1)}, bf16[64,1024]{1,0:T(8,128)(2,1)}, u32[]{:S(2)}, u32[]{:S(2)}) collective-permute-start(bf16[64,1024]{1,0:T(8,128)(2,1)S(1)} %concatenate.15), channel_id=1, source_target_pairs={{0,32},{4,36},{8,40},{12,44},{16,48},{20,52},{24,56},{28,60},{32,0... | collective-permute-start | bytes 393224 | tf_op jit(solution)/shard_map/ppermute | solution.py:42
  25.9 20.9 %collective-permute-start.2 = (f16[128,896]{0,1:T(8,128)(2,1)S(1)}, f16[128,896]{0,1:T(8,128)(2,1)S(1)}, u32[]{:S(2)}, u32[]{:S(2)}) collective-permute-start(f16[128,896]{0,1:T(8,128)(2,1)S(1)} %fusion.64), channel_id=1, source_target_pairs={{0,1},{1,2},{2,3},{3,0},{4,5},{5,6},{6,7},{7,4},{8,9},{9,10},{10,1... | collective-permute-start | bytes 688136 | tf_op jit(solution)/shard_map/ppermute | solution.py:18
  26.1 21.9 %collective-permute-start.5 = (f16[128,896]{0,1:T(8,128)(2,1)S(1)}, f16[128,896]{0,1:T(8,128)(2,1)S(1)}, u32[]{:S(2)}, u32[]{:S(2)}) collective-permute-start(f16[128,896]{0,1:T(8,128)(2,1)S(1)} %fusion.61), channel_id=1, source_target_pairs={{0,3},{1,0},{2,1},{3,2},{4,7},{5,4},{6,5},{7,6},{8,11},{9,8},{10,9... | collective-permute-start | bytes 688136 | tf_op jit(solution)/shard_map/ppermute | solution.py:18
  39.8 11.2 %collective-permute-start.18 = (bf16[2,32,1024]{2,1,0:T(8,128)(2,1)S(1)}, bf16[2,32,1024]{2,1,0:T(8,128)(2,1)S(1)}, u32[]{:S(2)}, u32[]{:S(2)}) collective-permute-start(bf16[2,32,1024]{2,1,0:T(8,128)(2,1)S(1)} %get-tuple-element.43), channel_id=1, source_target_pairs={{0,64},{4,68},{8,72},{12,76},{16,80},{20,84},{24,88},{28,92},{32,9... | collective-permute-start | bytes 393224 | tf_op jit(solution)/shard_map/ppermute | solution.py:42
  41.1 11.3 %collective-permute-start.17 = (bf16[2,32,1024]{2,1,0:T(8,128)(2,1)S(1)}, bf16[2,32,1024]{2,1,0:T(8,128)(2,1)S(1)}, u32[]{:S(2)}, u32[]{:S(2)}) collective-permute-start(bf16[2,32,1024]{2,1,0:T(8,128)(2,1)S(1)} %get-tuple-element.43), channel_id=1, source_target_pairs={{0,128},{4,132},{8,136},{12,140},{16,144},{20,148},{24,152},{28,15... | collective-permute-start | bytes 393224 | tf_op jit(solution)/shard_map/ppermute | solution.py:42
  43.5 9.0 %collective-permute-start.16 = (bf16[2,32,1024]{2,1,0:T(8,128)(2,1)S(1)}, bf16[2,32,1024]{2,1,0:T(8,128)(2,1)S(1)}, u32[]{:S(2)}, u32[]{:S(2)}) collective-permute-start(bf16[2,32,1024]{2,1,0:T(8,128)(2,1)S(1)} %get-tuple-element.43), channel_id=1, source_target_pairs={{0,192},{4,196},{8,200},{12,204},{16,208},{20,212},{24,216},{28,22... | collective-permute-start | bytes 393224 | tf_op jit(solution)/shard_map/ppermute | solution.py:42
  46.7 9.3 %collective-permute-start.15 = (bf16[2,32,1024]{2,1,0:T(8,128)(2,1)S(1)}, bf16[2,32,1024]{2,1,0:T(8,128)(2,1)S(1)}, u32[]{:S(2)}, u32[]{:S(2)}) collective-permute-start(bf16[2,32,1024]{2,1,0:T(8,128)(2,1)S(1)} %get-tuple-element.39), channel_id=1, source_target_pairs={{0,8},{4,12},{8,16},{12,20},{16,24},{20,28},{24,0},{28,4},{32,40},... | collective-permute-start | bytes 393224 | tf_op jit(solution)/shard_map/ppermute | solution.py:42
  52.4 11.5 %collective-permute-start.8 = (f16[448,256]{1,0:T(8,128)(2,1)S(1)}, f16[448,256]{1,0:T(8,128)(2,1)S(1)}, u32[]{:S(2)}, u32[]{:S(2)}) collective-permute-start(f16[448,256]{1,0:T(8,128)(2,1)S(1)} %get-tuple-element.70), channel_id=1, source_target_pairs={{0,1},{1,2},{2,3},{3,0},{4,5},{5,6},{6,7},{7,4},{8,9},{9,10},{10,1... | collective-permute-start | bytes 688136 | tf_op jit(solution)/shard_map/ppermute | solution.py:18
  52.5 16.6 %collective-permute-start.6 = (f16[448,256]{1,0:T(8,128)(2,1)S(1)}, f16[448,256]{1,0:T(8,128)(2,1)S(1)}, u32[]{:S(2)}, u32[]{:S(2)}) collective-permute-start(f16[448,256]{1,0:T(8,128)(2,1)S(1)} %get-tuple-element.70), channel_id=1, source_target_pairs={{0,3},{1,0},{2,1},{3,2},{4,7},{5,4},{6,5},{7,6},{8,11},{9,8},{10,9... | collective-permute-start | bytes 688136 | tf_op jit(solution)/shard_map/ppermute | solution.py:18
  56.1 20.5 %collective-permute-start.11 = (f16[448,256]{1,0:T(8,128)(2,1)S(1)}, f16[448,256]{1,0:T(8,128)(2,1)S(1)}, u32[]{:S(2)}, u32[]{:S(2)}) collective-permute-start(f16[448,256]{1,0:T(8,128)(2,1)S(1)} %get-tuple-element.71), channel_id=1, source_target_pairs={{0,1},{1,2},{2,3},{3,0},{4,5},{5,6},{6,7},{7,4},{8,9},{9,10},{10,1... | collective-permute-start | bytes 688136 | tf_op jit(solution)/shard_map/ppermute | solution.py:18
  56.1 18.5 %collective-permute-start.7 = (f16[448,256]{1,0:T(8,128)(2,1)S(1)}, f16[448,256]{1,0:T(8,128)(2,1)S(1)}, u32[]{:S(2)}, u32[]{:S(2)}) collective-permute-start(f16[448,256]{1,0:T(8,128)(2,1)S(1)} %get-tuple-element.71), channel_id=1, source_target_pairs={{0,3},{1,0},{2,1},{3,2},{4,7},{5,4},{6,5},{7,6},{8,11},{9,8},{10,9... | collective-permute-start | bytes 688136 | tf_op jit(solution)/shard_map/ppermute | solution.py:18
  59.7 29.5 %collective-permute-start.24 = (bf16[4,2,32,1024]{3,2,1,0:T(8,128)(2,1)S(1)}, bf16[4,2,32,1024]{3,2,1,0:T(8,128)(2,1)S(1)}, u32[]{:S(2)}, u32[]{:S(2)}) collective-permute-start(bf16[4,2,32,1024]{3,2,1,0:T(8,128)(2,1)S(1)} %pad_maximum_fusion.4), channel_id=1, source_target_pairs={{0,8},{4,12},{8,16},{12,20},{16,24},{20,28},{24,0},{28,4},{32,40},... | collective-permute-start | bytes 1572872 | tf_op jit(solution)/shard_map/ppermute | solution.py:42
  64.0 43.1 %collective-permute-start.23 = (bf16[4,2,32,1024]{3,2,1,0:T(8,128)(2,1)S(1)}, bf16[4,2,32,1024]{3,2,1,0:T(8,128)(2,1)S(1)}, u32[]{:S(2)}, u32[]{:S(2)}) collective-permute-start(bf16[4,2,32,1024]{3,2,1,0:T(8,128)(2,1)S(1)} %pad_maximum_fusion.4), channel_id=1, source_target_pairs={{0,16},{4,20},{8,24},{12,28},{16,0},{20,4},{24,8},{28,12},{32,48},... | collective-permute-start | bytes 1572872 | tf_op jit(solution)/shard_map/ppermute | solution.py:42
  69.1 38.0 %collective-permute-start.22 = (bf16[4,2,32,1024]{3,2,1,0:T(8,128)(2,1)S(1)}, bf16[4,2,32,1024]{3,2,1,0:T(8,128)(2,1)S(1)}, u32[]{:S(2)}, u32[]{:S(2)}) collective-permute-start(bf16[4,2,32,1024]{3,2,1,0:T(8,128)(2,1)S(1)} %pad_maximum_fusion.4), channel_id=1, source_target_pairs={{0,24},{4,28},{8,0},{12,4},{16,8},{20,12},{24,16},{28,20},{32,56},... | collective-permute-start | bytes 1572872 | tf_op jit(solution)/shard_map/ppermute | solution.py:42
  83.0 24.1 %collective-permute-start.21 = (bf16[4,2,32,1024]{3,2,1,0:T(8,128)(2,1)S(1)}, bf16[4,2,32,1024]{3,2,1,0:T(8,128)(2,1)}, u32[]{:S(2)}, u32[]{:S(2)}) collective-permute-start(bf16[4,2,32,1024]{3,2,1,0:T(8,128)(2,1)S(1)} %pad_maximum_fusion.3), channel_id=1, source_target_pairs={{0,64},{4,68},{8,72},{12,76},{16,80},{20,84},{24,88},{28,92},{32,9... | collective-permute-start | bytes 1572872 | tf_op jit(solution)/shard_map/ppermute | solution.py:42
  85.2 28.7 %collective-permute-start.20 = (bf16[4,2,32,1024]{3,2,1,0:T(8,128)(2,1)S(1)}, bf16[4,2,32,1024]{3,2,1,0:T(8,128)(2,1)}, u32[]{:S(2)}, u32[]{:S(2)}) collective-permute-start(bf16[4,2,32,1024]{3,2,1,0:T(8,128)(2,1)S(1)} %pad_maximum_fusion.3), channel_id=1, source_target_pairs={{0,128},{4,132},{8,136},{12,140},{16,144},{20,148},{24,152},{28,15... | collective-permute-start | bytes 1572872 | tf_op jit(solution)/shard_map/ppermute | solution.py:42
  89.3 29.4 %collective-permute-start.19 = (bf16[4,2,32,1024]{3,2,1,0:T(8,128)(2,1)S(1)}, bf16[4,2,32,1024]{3,2,1,0:T(8,128)(2,1)}, u32[]{:S(2)}, u32[]{:S(2)}) collective-permute-start(bf16[4,2,32,1024]{3,2,1,0:T(8,128)(2,1)S(1)} %pad_maximum_fusion.3), channel_id=1, source_target_pairs={{0,192},{4,196},{8,200},{12,204},{16,208},{20,212},{24,216},{28,22... | collective-permute-start | bytes 1572872 | tf_op jit(solution)/shard_map/ppermute | solution.py:42
  92.5 52.0 %all-to-all-start = ((bf16[64,56,256]{2,1,0:T(8,128)(2,1)}), bf16[64,56,256]{2,1,0:T(8,128)(2,1)}, u32[]{:S(2)}, u32[]{:S(2)}) async-start(bf16[64,56,256]{2,1,0:T(8,128)(2,1)} %bitcast.5), calls=%async_computation | async-start | bytes 3670016 | tf_op jit(solution)/shard_map/all_to_all | solution.py:282
  120.4 15.8 %collective-permute-start.25 = (bf16[4,4,2,32,1024]{4,3,2,1,0:T(8,128)(2,1)S(1)}, bf16[4,4,2,32,1024]{4,3,2,1,0:T(8,128)(2,1)}, u32[]{:S(2)}, u32[]{:S(2)}) collective-permute-start(bf16[4,4,2,32,1024]{4,3,2,1,0:T(8,128)(2,1)S(1)} %pad_maximum_fusion), channel_id=1, source_target_pairs={{0,4},{4,0},{8,12},{12,8},{16,20},{20,16},{24,28},{28,24},{32,36},... | collective-permute-start | bytes 6291464 | tf_op jit(solution)/shard_map/ppermute | solution.py:42
  132.2 8.8 %collective-permute-start.26 = (bf16[4,4,2,32,1024]{4,3,2,1,0:T(8,128)(2,1)}, bf16[4,4,2,32,1024]{4,3,2,1,0:T(8,128)(2,1)}, u32[]{:S(2)}, u32[]{:S(2)}) collective-permute-start(bf16[4,4,2,32,1024]{4,3,2,1,0:T(8,128)(2,1)} %pad_maximum_fusion.1), channel_id=1, source_target_pairs={{0,4},{4,0},{8,12},{12,8},{16,20},{20,16},{24,28},{28,24},{32,36},... | collective-permute-start | bytes 6291464 | tf_op jit(solution)/shard_map/ppermute | solution.py:42
  (14 other events, 136.0 us)
